TPU v7x, 512 devices: a whole 4x8x8 slice. The times are simulated.
512 devices in a mesh: grp: 8 (over y), row: 64 (over z, x, core).
Axes of the slice: x: 4, y: 8, z: 8, core: 2. Of those that a mesh axis runs over, the one named last changes fastest.
Arguments:
- embeddings: bfloat16 [262144, 768], P(('grp', 'row')), may hold values from -2000 to 2000
Outputs:
- whitened: bfloat16 [262144, 768], P(('grp', 'row'))
- energy: float32 [], replicated
All inputs are finite; a program needn't handle non-finite values.
Results may differ from a plain program's by a relative error of at most 0.0007.
The roundings to bfloat16 on the way count: a program that leaves them out, or rounds other values in their place, can miss the bound.
Values may be sent and summed in bfloat16 or wider, within the bound.
No kernel may reach another device: no remote copies, remote signals or barrier semaphores. Data moves between devices by JAX's collectives and lax.ppermute only.
A program may use at most 64 MiB of HBM per device.

v0:
```python
import jax
import jax.numpy as jnp
from jax import lax
from jax.sharding import Mesh
from jax.sharding import PartitionSpec as P

ITERS = 4
ROW = ("row_0", "row_1", "row_2")
GRP_ROW = ("grp", "row_0", "row_1", "row_2")


def split_up(array, dim, peers):
    dims = array.shape
    parts = array.reshape(*dims[:dim], peers, dims[dim] // peers, *dims[dim + 1 :])
    return jnp.moveaxis(parts, dim, 0)


def summed_on_arrival(array, axis, dim):
    peers = lax.axis_size(axis)
    parts = lax.all_to_all(split_up(array, dim, peers), axis, 0, 0, tiled=True)
    return jnp.sum(parts, axis=0)


def sum_in_two_steps(array, axes, dim):
    far, near = axes
    parts = split_up(array, dim, lax.axis_size(far))
    nearer = summed_on_arrival(parts, near, dim + 1)
    arrived = lax.all_to_all(nearer, far, split_axis=0, concat_axis=0, tiled=True)
    return arrived.sum(axis=0)


def from_everyone(array, axis):
    peers = lax.axis_size(axis)
    return lax.all_to_all(
        jnp.broadcast_to(array[None], (peers, *array.shape)), axis, 0, 0, tiled=True
    )


def of_everyone(array, axis):
    everything = from_everyone(array, axis)
    return jnp.sum(everything, axis=0)


def by_axis(array, axes):
    far, near = axes
    return of_everyone(of_everyone(array, near), far)


def in_order(parts, dim):
    parts = jnp.moveaxis(parts, 0, dim)
    dims = parts.shape
    return parts.reshape(*dims[:dim], dims[dim] * dims[dim + 1], *dims[dim + 2 :])


def gather_axes(array, axes, dim):
    far, near = axes
    initial = from_everyone(array, far)
    parts = jnp.swapaxes(from_everyone(initial, near), 0, 1)
    return in_order(parts.reshape(-1, *array.shape), dim)


def stacked_from(array, axes, sequence):
    parts = array
    for k in sequence:
        parts = lax.all_gather(parts, axes[k])
    done = sequence[::-1]
    back = [done.index(k) for k in range(len(axes))]
    parts = parts.transpose(*back, *range(len(axes), parts.ndim))
    return parts.reshape(-1, *array.shape)


def gathered_by_axis(array, axes, sequence, dim):
    return in_order(stacked_from(array, axes, sequence), dim)


def local(embeddings):
    rows_dev = embeddings.shape[0]
    width = embeddings.shape[1]
    n_row = lax.axis_size(ROW)
    slab = width // n_row
    rows_total = rows_dev * lax.axis_size("grp") * n_row
    first = lax.axis_index(ROW) * slab
    colsum = jnp.sum(embeddings, axis=0, dtype=jnp.float32)
    contract = (((0,), (0,)), ((), ()))
    group_rows = sum_in_two_steps(
        lax.dot_general(embeddings, embeddings, contract, preferred_element_type=jnp.float32),
        (("row_0", "row_1"), "row_2"),
        0,
    )
    second_rows = of_everyone(group_rows, "grp")
    total = by_axis(colsum, (("grp", "row_0"), ("row_1", "row_2")))
    mean = total / rows_total
    mean_rows = lax.dynamic_slice_in_dim(mean, first, slab, 0)
    cov_rows = second_rows / rows_total - mean_rows[:, None] * mean[None, :]
    squares = of_everyone(jnp.sum(cov_rows * cov_rows), ROW)
    fro = jnp.sqrt(squares + 1e-06)
    scaled_rows = cov_rows / fro
    row_ids = lax.broadcasted_iota(jnp.int32, (slab, width), 0) + first
    col_ids = lax.broadcasted_iota(jnp.int32, (slab, width), 1)
    eye_rows = (row_ids == col_ids).astype(jnp.float32)
    hp = lax.Precision.HIGHEST
    iterate_rows = 1.5 * eye_rows - 0.5 * scaled_rows
    for step in range(ITERS - 1):
        iterate_full = gather_axes(iterate_rows, (("row_0", "row_1"), "row_2"), 0)
        prod = jnp.dot(scaled_rows, iterate_full, precision=hp)
        prod = jnp.dot(prod, iterate_full, precision=hp)
        prod = jnp.dot(prod, iterate_full, precision=hp)
        iterate_rows = 1.5 * iterate_rows - 0.5 * prod
    transform_rows = (iterate_rows / jnp.sqrt(fro)).astype(jnp.bfloat16)
    centered = (embeddings.astype(jnp.float32) - mean).astype(jnp.bfloat16)
    product = lax.dot_general(
        centered,
        gathered_by_axis(transform_rows, ROW, (1, 0, 2), 0),
        (((1,), (1,)), ((), ())),
        preferred_element_type=jnp.float32,
    )
    energy = by_axis(jnp.sum(product * product), (("grp", "row_0"), ("row_1", "row_2"))) / (
        rows_total * width
    )
    return (product.astype(jnp.bfloat16), energy)


def solution(mesh):
    torus = Mesh(
        mesh.devices.reshape(mesh.shape["grp"], 8, 4, 2), ("grp", "row_0", "row_1", "row_2")
    )
    in_specs = (P(GRP_ROW, None),)
    out_specs = (P(GRP_ROW, None), P())
    return jax.shard_map(local, mesh=torus, in_specs=in_specs, out_specs=out_specs, check_vma=False)
```

profile of v0, /device:TPU:1, one launch (start us, length us, event | category | flops | bytes accessed | tf_op | source)
XLA Modules:
  0.0 427.4 jit_solution(6484216506768823939)
XLA Ops:
  7.2 2.2 fusion.17
  9.4 1.8 reshape_reshape.15
  11.2 4.7 %copy.51 = f32[2,32,12,768]{3,1,2,0:T(8,128)} copy(f32[2,32,12,768]{3,2,0,1:T(8,128)} %bitcast.30) | data formatting | bytes 4718592 | tf_op jit(solution)/shard_map/transpose | solution.py:15
  15.9 10.8 %all-to-all-start.2 = ((f32[2,32,12,768]{3,1,2,0:T(8,128)}), f32[2,32,12,768]{3,1,2,0:T(8,128)S(1)}, u32[]{:S(2)}, u32[]{:S(2)}) async-start(f32[2,32,12,768]{3,1,2,0:T(8,128)} %copy.51), calls=%async_computation.2 | async-start | bytes 4718592 | tf_op jit(solution)/shard_map/all_to_all | solution.py:20
  26.8 2.5 all-to-all-done.2
  29.9 3.6 all-to-all-start
  33.6 1.3 reduce_sum.102
  34.8 3.1 copy.52
  38.3 8.4 %all-to-all-start.3 = ((f32[32,12,768]{2,1,0:T(8,128)}), f32[32,12,768]{2,1,0:T(8,128)S(1)}, u32[]{:S(2)}, u32[]{:S(2)}) async-start(f32[32,12,768]{2,1,0:T(8,128)} %copy.52), calls=%async_computation.3 | async-start | bytes 3145728 | tf_op jit(solution)/shard_map/all_to_all | solution.py:28
  46.7 37.7 %all-to-all-done.3 = f32[32,12,768]{2,1,0:T(8,128)S(1)} async-done(((f32[32,12,768]{2,1,0:T(8,128)}), f32[32,12,768]{2,1,0:T(8,128)S(1)}, u32[]{:S(2)}, u32[]{:S(2)}) %all-to-all-start.3) | async-done | bytes 1179680 | tf_op jit(solution)/shard_map/all_to_all | solution.py:28
  85.2 9.4 %all-to-all-start.1 = ((f32[64,1,768]{2,1,0:T(1,128)}), f32[64,1,768]{2,1,0:T(1,128)S(1)}, u32[]{:S(2)}, u32[]{:S(2)}) async-start(f32[64,1,768]{2,1,0:T(1,128)} %broadcast_in_dim.25), calls=%async_computation.1 | async-start | bytes 393216 | tf_op jit(solution)/shard_map/all_to_all | solution.py:34
  94.7 11.8 %all-to-all-done.1 = f32[64,1,768]{2,1,0:T(1,128)S(1)} async-done(((f32[64,1,768]{2,1,0:T(1,128)}), f32[64,1,768]{2,1,0:T(1,128)S(1)}, u32[]{:S(2)}, u32[]{:S(2)}) %all-to-all-start.1) | async-done | bytes 196640 | tf_op jit(solution)/shard_map/all_to_all | solution.py:34
  107.3 3.5 all-to-all-start.4
  111.0 10.5 %all-to-all-done.4 = f32[8,12,768]{2,1,0:T(8,128)S(1)} async-done(((f32[8,12,768]{2,1,0:T(8,128)}), f32[8,12,768]{2,1,0:T(8,128)S(1)}, u32[]{:S(2)}, u32[]{:S(2)}) %all-to-all-start.4) | async-done | bytes 294944 | tf_op jit(solution)/shard_map/all_to_all | solution.py:34
  122.3 1.3 broadcast_in_dim.27
  123.5 11.0 %all-to-all-start.5 = ((f32[64,1,1]{2,1,0:T(1,128)}), f32[64,1,1]{2,1,0:T(1,128)S(1)}, u32[]{:S(2)}, u32[]{:S(2)}) async-start(f32[64,1,1]{2,1,0:T(1,128)} %broadcast_in_dim.27), calls=%async_computation.5 | async-start | bytes 65536 | tf_op jit(solution)/shard_map/all_to_all | solution.py:34
  134.5 9.3 %all-to-all-done.5 = f32[64,1,1]{2,1,0:T(1,128)S(1)} async-done(((f32[64,1,1]{2,1,0:T(1,128)}), f32[64,1,1]{2,1,0:T(1,128)S(1)}, u32[]{:S(2)}, u32[]{:S(2)}) %all-to-all-start.5) | async-done | bytes 288 | tf_op jit(solution)/shard_map/all_to_all | solution.py:34
  145.5 41.7 %all_to_all.75 = f32[32,12,768]{2,1,0:T(8,128)S(1)} all-to-all(f32[32,12,768]{2,1,0:T(8,128)S(1)} %broadcast_in_dim.28), channel_id=1, replica_groups=mesh['grp'=8,'row_0'=8,'row_1'=4,'row_2'=2] {'row_0','row_1'}, dimensions={0} | all-to-all | bytes 2359296 | tf_op jit(solution)/shard_map/all_to_all | solution.py:34
  188.1 7.9 %all_to_all.76 = f32[2,32,12,768]{3,1,2,0:T(8,128)S(1)} all-to-all(f32[2,32,12,768]{3,1,2,0:T(8,128)S(1)} %broadcast_in_dim.29), channel_id=1, replica_groups=mesh['grp'=8,'row_0'=8,'row_1'=4,'row_2'=2] {'row_2'}, dimensions={0} | all-to-all | bytes 4718592 | tf_op jit(solution)/shard_map/all_to_all | solution.py:34
  196.0 3.1 copy.56
  199.1 2.6 reshape_reshape.16
  201.7 1.2 fusion.15
  202.9 1.2 fusion.18
  204.2 1.2 fusion.4
  205.6 43.1 %all_to_all.77 = f32[32,12,768]{2,1,0:T(8,128)S(1)} all-to-all(f32[32,12,768]{2,1,0:T(8,128)S(1)} %broadcast_in_dim.30), channel_id=1, replica_groups=mesh['grp'=8,'row_0'=8,'row_1'=4,'row_2'=2] {'row_0','row_1'}, dimensions={0} | all-to-all | bytes 2359296 | tf_op jit(solution)/shard_map/all_to_all | solution.py:34
  249.6 7.5 %all_to_all.78 = f32[2,32,12,768]{3,1,2,0:T(8,128)S(1)} all-to-all(f32[2,32,12,768]{3,1,2,0:T(8,128)S(1)} %broadcast_in_dim.31), channel_id=1, replica_groups=mesh['grp'=8,'row_0'=8,'row_1'=4,'row_2'=2] {'row_2'}, dimensions={0} | all-to-all | bytes 4718592 | tf_op jit(solution)/shard_map/all_to_all | solution.py:34
  257.1 3.1 copy.58
  260.1 2.6 reshape_reshape.17
  262.8 1.2 fusion.13
  264.0 1.2 fusion.19
  265.2 1.2 fusion.3
  266.4 1.3 broadcast_in_dim.32
  267.8 4.4 %all-to-all-start.10 = ((f32[32,12,768]{2,1,0:T(8,128)}), f32[32,12,768]{2,1,0:T(8,128)S(1)}, u32[]{:S(2)}, u32[]{:S(2)}) async-start(f32[32,12,768]{2,1,0:T(8,128)} %broadcast_in_dim.32), calls=%async_computation.10 | async-start | bytes 3145728 | tf_op jit(solution)/shard_map/all_to_all | solution.py:34
  272.2 37.7 %all-to-all-done.10 = f32[32,12,768]{2,1,0:T(8,128)S(1)} async-done(((f32[32,12,768]{2,1,0:T(8,128)}), f32[32,12,768]{2,1,0:T(8,128)S(1)}, u32[]{:S(2)}, u32[]{:S(2)}) %all-to-all-start.10) | async-done | bytes 1179680 | tf_op jit(solution)/shard_map/all_to_all | solution.py:34
  310.8 7.7 %all_to_all.79 = f32[2,32,12,768]{3,1,2,0:T(8,128)S(1)} all-to-all(f32[2,32,12,768]{3,1,2,0:T(8,128)S(1)} %broadcast_in_dim.33), channel_id=1, replica_groups=mesh['grp'=8,'row_0'=8,'row_1'=4,'row_2'=2] {'row_2'}, dimensions={0} | all-to-all | bytes 4718592 | tf_op jit(solution)/shard_map/all_to_all | solution.py:34
  318.6 3.1 copy.60
  321.6 2.6 reshape_reshape.18
  324.3 1.2 fusion.11
  325.5 1.2 fusion.20
  326.7 1.2 fusion.6
  327.9 9.9 %all-gather.3 = bf16[4,12,768]{2,1,0:T(8,128)(2,1)S(1)} all-gather(bf16[1,12,768]{2,1,0:T(8,128)(2,1)S(1)} %fusion.6), channel_id=2, replica_groups=mesh['grp'=8,'row_0'=8,'row_1'=4,'row_2'=2] {'row_1'}, dimensions={0}, use_global_device_ids=true | all-gather | bytes 92160 | tf_op jit(solution)/shard_map/all_gather | solution.py:65
  337.8 20.8 %all-gather.1 = bf16[32,12,768]{2,1,0:T(8,128)(2,1)S(1)} all-gather(bf16[4,12,768]{2,1,0:T(8,128)(2,1)S(1)} %all-gather.3), channel_id=3, replica_groups=mesh['grp'=8,'row_0'=8,'row_1'=4,'row_2'=2] {'row_0'}, dimensions={0}, use_global_device_ids=true | all-gather | bytes 663552 | tf_op jit(solution)/shard_map/all_gather | solution.py:65
  359.7 18.3 %all-gather.6.cloned.1.call-done = bf16[16,4,12,768]{3,1,0,2:T(4,128)(2,1)} async-done(((bf16[8,4,12,768]{3,1,0,2:T(4,128)(2,1)}), bf16[16,4,12,768]{3,1,0,2:T(4,128)(2,1)}) %all-gather.6.cloned.1.call-update) | async-done | bytes 1179664 | tf_op jit(solution)/shard_map/all_gather | solution.py:65
  378.1 1.4 copy.74
  379.9 1.2 reshape_reshape.19
  381.0 3.6 multiply_reduce_fusion
  385.3 7.9 %all_to_all.80 = f32[8,1,1]{2,1,0:T(1,128)S(1)} all-to-all(f32[8,1,1]{2,1,0:T(1,128)S(1)} %broadcast_in_dim.34), channel_id=1, replica_groups=mesh['grp'=8,'row_0'=8,'row_1'=4,'row_2'=2] {'row_1','row_2'}, dimensions={0} | all-to-all | bytes 64 | tf_op jit(solution)/shard_map/all_to_all | solution.py:34
  394.4 23.7 %all_to_all.81 = f32[64,1,1]{2,1,0:T(1,128)S(1)} all-to-all(f32[64,1,1]{2,1,0:T(1,128)S(1)} %broadcast_in_dim.35), channel_id=1, replica_groups=mesh['grp'=8,'row_0'=8,'row_1'=4,'row_2'=2] {'grp','row_0'}, dimensions={0} | all-to-all | bytes 512 | tf_op jit(solution)/shard_map/all_to_all | solution.py:34
  (33 shorter events, 11.8 us)
Async XLA Ops:
  15.9 10.8 %copy-start = (bf16[512,768]{1,0:T(8,128)(2,1)S(1)}, bf16[512,768]{1,0:T(8,128)(2,1)}, u32[]{:S(2)}) copy-start(bf16[512,768]{1,0:T(8,128)(2,1)} %param.1) | copy-start | bytes 2359300
  15.9 13.5 %all-to-all-start.2 = ((f32[2,32,12,768]{3,1,2,0:T(8,128)}), f32[2,32,12,768]{3,1,2,0:T(8,128)S(1)}, u32[]{:S(2)}, u32[]{:S(2)}) async-start(f32[2,32,12,768]{3,1,2,0:T(8,128)} %copy.51), calls=%async_computation.2 | async-start | bytes 4718592 | tf_op jit(solution)/shard_map/all_to_all | solution.py:20
  29.9 8.3 %all-to-all-start = ((f32[8,1,768]{2,1,0:T(1,128)}), f32[8,1,768]{2,1,0:T(1,128)S(1)}, u32[]{:S(2)}, u32[]{:S(2)}) async-start(f32[8,1,768]{2,1,0:T(1,128)} %broadcast_in_dim.24), calls=%async_computation | async-start | bytes 49152 | tf_op jit(solution)/shard_map/all_to_all | solution.py:34
  38.3 46.2 %all-to-all-start.3 = ((f32[32,12,768]{2,1,0:T(8,128)}), f32[32,12,768]{2,1,0:T(8,128)S(1)}, u32[]{:S(2)}, u32[]{:S(2)}) async-start(f32[32,12,768]{2,1,0:T(8,128)} %copy.52), calls=%async_computation.3 | async-start | bytes 3145728 | tf_op jit(solution)/shard_map/all_to_all | solution.py:28
  85.2 21.4 %all-to-all-start.1 = ((f32[64,1,768]{2,1,0:T(1,128)}), f32[64,1,768]{2,1,0:T(1,128)S(1)}, u32[]{:S(2)}, u32[]{:S(2)}) async-start(f32[64,1,768]{2,1,0:T(1,128)} %broadcast_in_dim.25), calls=%async_computation.1 | async-start | bytes 393216 | tf_op jit(solution)/shard_map/all_to_all | solution.py:34
  107.3 14.2 %all-to-all-start.4 = ((f32[8,12,768]{2,1,0:T(8,128)}), f32[8,12,768]{2,1,0:T(8,128)S(1)}, u32[]{:S(2)}, u32[]{:S(2)}) async-start(f32[8,12,768]{2,1,0:T(8,128)} %broadcast_in_dim.26), calls=%async_computation.4 | async-start | bytes 786432 | tf_op jit(solution)/shard_map/all_to_all | solution.py:34
  123.5 20.3 %all-to-all-start.5 = ((f32[64,1,1]{2,1,0:T(1,128)}), f32[64,1,1]{2,1,0:T(1,128)S(1)}, u32[]{:S(2)}, u32[]{:S(2)}) async-start(f32[64,1,1]{2,1,0:T(1,128)} %broadcast_in_dim.27), calls=%async_computation.5 | async-start | bytes 65536 | tf_op jit(solution)/shard_map/all_to_all | solution.py:34
  267.8 42.1 %all-to-all-start.10 = ((f32[32,12,768]{2,1,0:T(8,128)}), f32[32,12,768]{2,1,0:T(8,128)S(1)}, u32[]{:S(2)}, u32[]{:S(2)}) async-start(f32[32,12,768]{2,1,0:T(8,128)} %broadcast_in_dim.32), calls=%async_computation.10 | async-start | bytes 3145728 | tf_op jit(solution)/shard_map/all_to_all | solution.py:34
  272.2 105.9 %all-gather.6.cloned.1.call-start = ((), (), s32[]{:S(2)}) async-start(), calls=%async_computation.14 | async-start | bytes 1769472 | tf_op jit(solution)/shard_map/all_gather | solution.py:65
Sparse Core Ops, SparseCore 0:
  359.8 18.1 all-gather.5
where the time goes:
time: 429 us; the launch traced here: 427 us
  blocking collectives  170 us (40%)
  waiting for transfers between devices  128 us (30%)
  starting transfers between devices  51.1 us (12%)
  local copies, waits for them, and re-layouts  40.1 us (9%)
  matrix products  16.8 us (4%)
  between operations  16.7 us (4%)
  other arithmetic  4.46 us (1%)
    all_to_all x7, blocking collectives, from_everyone(): lax.all_to_all(jnp.broadcast_to(array[None], (peers, *array.shape)), axis...  139 us
    all_to_all x5, waiting for transfers between devices, from_everyone(): lax.all_to_all(jnp.broadcast_to(array[None], (peers, *array.shape)), axis...  69.6 us
    all_to_all x1, waiting for transfers between devices, sum_in_two_steps(): lax.all_to_all(nearer, far, split_axis=0, concat_axis=0, tiled=True)  37.7 us
    all_to_all x5, starting transfers between devices, from_everyone(): lax.all_to_all(jnp.broadcast_to(array[None], (peers, *array.shape)), axis...  31.8 us
    all_gather x2, blocking collectives, stacked_from(): parts = lax.all_gather(parts, axes[k])  30.6 us
    all_gather x1, waiting for transfers between devices, stacked_from(): parts = lax.all_gather(parts, axes[k])  18.3 us
    all_to_all x1, starting transfers between devices, summed_on_arrival(): parts = lax.all_to_all(split_up(array, dim, peers), axis, 0, 0, tiled=True)  10.8 us
    transpose x3, local copies, waits for them, and re-layouts, gather_axes(): parts = jnp.swapaxes(from_everyone(initial, near), 0, 1)  9.2 us
  transfers between devices with their start and end apart: 8, of which 8 were waited for; matrix products, arithmetic and copies ran while one was open for 1% of the time, Pallas kernels for 0%

commit v1 on v0

v1 whole, which is shorter than its diff:
```python
import functools

import jax
import jax.numpy as jnp
from jax import lax
from jax.experimental import pallas as pl
from jax.experimental.pallas import tpu as pltpu
from jax.sharding import Mesh
from jax.sharding import PartitionSpec as P

ITERS = 4
AXES = ("grp", "row_0", "row_1", "row_2")
LANES = 128
TILE = 256
F32 = jnp.float32
BF16 = jnp.bfloat16


def layout(width):
    nb = width // LANES
    off = {}
    at = 0
    for i in range(nb):
        for j in range(i + 1, nb):
            off[i, j] = at
            at += LANES
    merged = {}
    for i in range(0, nb, 2):
        merged[i] = at
        at += LANES
    return nb, off, merged, at


def upper(shape):
    r = lax.broadcasted_iota(jnp.int32, shape, 0)
    c = lax.broadcasted_iota(jnp.int32, shape, 1)
    return r <= c, r == c


def gram_kernel(e_ref, o_ref):
    width = e_ref.shape[1]
    nb, off, merged, tail = layout(width)
    e = e_ref[...]
    keep, diag = upper((LANES, LANES))
    diagonal = {}
    lines = []
    for big in range(0, width, TILE):
        g = lax.dot_general(
            e[:, big : big + TILE], e[:, big:], (((0,), (0,)), ((), ())), preferred_element_type=F32
        )
        for i in range(big // LANES, (big + TILE) // LANES):
            r = i * LANES - big
            for j in range(i, nb):
                block = g[r : r + LANES, j * LANES - big : (j + 1) * LANES - big]
                if i == j:
                    diagonal[i] = block
                else:
                    o_ref[off[i, j] : off[i, j] + LANES, :] = block
        i = big // LANES
        a, b = diagonal[i], diagonal[i + 1]
        o_ref[merged[i] : merged[i] + LANES, :] = jnp.where(keep, a, b)
        lines.append(jnp.sum(jnp.where(diag, b, 0.0), axis=0, keepdims=True))
    colsum = jnp.sum(e.astype(F32), axis=0, keepdims=True)
    o_ref[tail:, :] = jnp.zeros((o_ref.shape[0] - tail, LANES), F32)
    for k in range(nb):
        o_ref[tail + k : tail + k + 1, :] = colsum[:, k * LANES : (k + 1) * LANES]
    for k, line in enumerate(lines):
        o_ref[tail + nb + k : tail + nb + k + 1, :] = line


def total_kernel(piece, x_ref, o_ref):
    period = 8 * piece
    groups = x_ref.shape[0] // period
    acc = jnp.sum(x_ref[...].reshape(groups, period, LANES), axis=0)
    for shift in (piece, 2 * piece, 4 * piece):
        acc = acc + jnp.concatenate([acc[period - shift :], acc[: period - shift]], axis=0)
    for g in range(groups):
        o_ref[g * period : (g + 1) * period, :] = acc


def split(x):
    hi = x.astype(BF16)
    lo = (x - hi.astype(F32)).astype(BF16)
    return hi, lo


def whiten_kernel(rows_total, e_ref, p_ref, o_ref, en_ref, s_ref, r_ref, q_ref, sh, sl, ah, al, bh, bl, w_ref):
    rows_dev, width = e_ref.shape
    nb, off, merged, tail = layout(width)
    inv = 1.0 / rows_total
    keep, diag = upper((LANES, LANES))
    means = [p_ref[tail + k : tail + k + 1, :] * inv for k in range(nb)]
    down = [jnp.transpose(jnp.broadcast_to(m, (LANES, LANES))) for m in means]

    squares = jnp.zeros((LANES, LANES), F32)
    for i in range(nb):
        for j in range(i, nb):
            if i != j:
                block = p_ref[off[i, j] : off[i, j] + LANES, :]
            else:
                base = i - i % 2
                packed = p_ref[merged[base] : merged[base] + LANES, :]
                mirror = jnp.transpose(packed)
                if i == base:
                    block = jnp.where(keep, packed, mirror)
                else:
                    line = p_ref[tail + nb + base // 2 : tail + nb + base // 2 + 1, :]
                    block = jnp.where(diag, line, jnp.where(keep, mirror, packed))
            cov = block * inv - down[i] * means[j]
            squares = squares + (cov * cov) * (1.0 if i == j else 2.0)
            s_ref[i * LANES : (i + 1) * LANES, j * LANES : (j + 1) * LANES] = cov
    total = jnp.sum(jnp.sum(squares, axis=0, keepdims=True), axis=1, keepdims=True)
    fro = jnp.sqrt(total + 1e-06)
    rescale = 1.0 / fro
    for i in range(nb):
        for j in range(i, nb):
            at = (slice(i * LANES, (i + 1) * LANES), slice(j * LANES, (j + 1) * LANES))
            s = s_ref[at] * rescale
            s_ref[at] = s
            sh[at], sl[at] = split(s)
            if i != j:
                turned = jnp.transpose(s)
                ta = (at[1], at[0])
                sh[ta], sl[ta] = split(turned)
                if i // (TILE // LANES) == j // (TILE // LANES):
                    s_ref[ta] = turned

    nt = width // TILE
    pairs = [(i, j) for i in range(nt) for j in range(i, nt)]

    def span(i):
        return slice(i * TILE, (i + 1) * TILE)

    def dot(a, b):
        return jnp.dot(a, b, preferred_element_type=F32)

    def product(xh, xl, yh, yl, i, j):
        a, b = span(i), span(j)
        return dot(xh[a, :], yh[:, b]) + (dot(xh[a, :], yl[:, b]) + dot(xl[a, :], yh[:, b]))

    def put(h_ref, l_ref, i, j, x):
        h_ref[span(i), span(j)], l_ref[span(i), span(j)] = split(x)
        if i != j:
            h_ref[span(j), span(i)], l_ref[span(j), span(i)] = split(jnp.transpose(x))

    def double_step(t_ref, th, tl, x_ref):
        for i, j in pairs:
            at = (span(i), span(j))
            t2 = product(th, tl, th, tl, i, j)
            t = t_ref[at]
            put(ah, al, i, j, t2)
            put(bh, bl, i, j, 0.0625 * t2 - 0.5625 * t)
            x_ref[at] = 1.6875 * t2 - 2.4375 * t
        for i, j in pairs:
            at = (span(i), span(j))
            x_ref[at] = x_ref[at] + product(ah, al, bh, bl, i, j)

    double_step(s_ref, sh, sl, r_ref)
    for i, j in pairs:
        put(ah, al, i, j, r_ref[span(i), span(j)])
    for i, j in pairs:
        at = (span(i), span(j))
        put(bh, bl, i, j, 4.5 * r_ref[at] + product(ah, al, ah, al, i, j))
    for i, j in pairs:
        at = (span(i), span(j))
        q_ref[at] = 5.0625 * s_ref[at] + product(sh, sl, bh, bl, i, j)
    for i, j in pairs:
        put(sh, sl, i, j, q_ref[span(i), span(j)])
    double_step(q_ref, sh, sl, q_ref)
    for i, j in pairs:
        put(ah, al, i, j, r_ref[span(i), span(j)])
        put(bh, bl, i, j, q_ref[span(i), span(j)])
    root = lax.rsqrt(fro)
    one = upper((TILE, TILE))[1]
    for i, j in pairs:
        at = (span(i), span(j))
        z = 2.25 * (r_ref[at] + q_ref[at]) + product(ah, al, bh, bl, i, j)
        if i == j:
            z = z + jnp.where(one, 5.0625, 0.0)
        w = (z * root).astype(BF16)
        w_ref[at] = w
        if i != j:
            w_ref[span(j), span(i)] = jnp.transpose(w.astype(F32)).astype(BF16)

    acc = jnp.zeros((TILE, TILE), F32)
    for i, j in pairs:
        g = dot(w_ref[span(i), :], w_ref[:, span(j)])
        acc = acc + g * s_ref[span(i), span(j)] * (1.0 if i == j else 2.0)
    trace = jnp.sum(jnp.sum(acc, axis=0, keepdims=True), axis=1, keepdims=True)
    en_ref[...] = trace * fro * (1.0 / width)

    mean = jnp.concatenate(means, axis=1)
    for r in range(0, rows_dev, TILE):
        c = (e_ref[r : r + TILE, :].astype(F32) - mean).astype(BF16)
        o_ref[r : r + TILE, :] = dot(c, w_ref[...]).astype(BF16)


def local(embeddings):
    rows_dev, width = embeddings.shape
    peers = lax.axis_size(AXES)
    rows_total = rows_dev * peers
    _, _, _, tail = layout(width)
    piece = -(-(tail + 16) // peers)
    rows = piece * peers
    packed_type = jax.ShapeDtypeStruct((rows, LANES), F32)
    vmem = pl.BlockSpec(memory_space=pltpu.VMEM)

    def exchange(x):
        x = x.reshape(peers, 1, piece * LANES)
        return lax.all_to_all(x, AXES, 0, 0, tiled=True).reshape(rows, LANES)

    packed = pl.pallas_call(gram_kernel, out_shape=packed_type, in_specs=[vmem], out_specs=vmem, name="gram")(embeddings)
    summed = pl.pallas_call(
        functools.partial(total_kernel, piece), out_shape=packed_type, in_specs=[vmem], out_specs=vmem, name="total"
    )(exchange(packed))
    everything = exchange(summed)
    square = (width, width)
    whitened, energy = pl.pallas_call(
        functools.partial(whiten_kernel, rows_total),
        out_shape=(jax.ShapeDtypeStruct((rows_dev, width), BF16), jax.ShapeDtypeStruct((1, 1), F32)),
        in_specs=[vmem, vmem],
        out_specs=(vmem, vmem),
        scratch_shapes=[pltpu.VMEM(square, F32)] * 3 + [pltpu.VMEM(square, BF16)] * 7,
        name="whiten",
    )(embeddings, everything)
    return whitened, energy.reshape(())


def solution(mesh):
    torus = Mesh(mesh.devices.reshape(mesh.shape["grp"], 8, 4, 2), AXES)
    return jax.shard_map(
        local, mesh=torus, in_specs=(P(AXES, None),), out_specs=(P(AXES, None), P()), check_vma=False
    )
```

time: 429 us -> 133 us (0.31)
  waiting for transfers between devices: 128 us -> 0 us
  blocking collectives: 170 us -> 108 us
  starting transfers between devices: 51.1 us -> 0 us
  local copies, waits for them, and re-layouts: 40.1 us -> 0 us
  Pallas kernels: 0 us -> 23.3 us
  matrix products: 16.8 us -> 0 us
  between operations: 16.7 us -> 0.63 us
  other arithmetic: 4.46 us -> 0 us
    all_to_all x7 -> x0, waiting for transfers between devices: 110 us -> none  [the longest x5 69.6 us: from_everyone(): lax.all_to_all(jnp.broadcast_to(array[None], (peers, *array.shape)), axis...]
    all_to_all x7 -> x0, starting transfers between devices: 51 us -> none  [the longest x5 31.8 us: from_everyone(): lax.all_to_all(jnp.broadcast_to(array[None], (peers, *array.shape)), axis...]
    all_to_all x7 -> x2, blocking collectives: 139 us -> 108 us  [exchange(): return lax.all_to_all(x, AXES, 0, 0, tiled=True).reshape(rows, LANES)]
    all_gather x2 -> x0, blocking collectives: 30.6 us -> none  [stacked_from(): parts = lax.all_gather(parts, axes[k])]
    pallas_call x0 -> x3, Pallas kernels: none -> 23.3 us  [the longest x1 17.9 us: local(): pl.pallas_call(functools.partial(whiten_kernel, rows_total), out_shape=(j...]
    all_gather x1 -> x0, waiting for transfers between devices: 18.3 us -> none  [stacked_from(): parts = lax.all_gather(parts, axes[k])]
    dot_general x11 -> x0, matrix products: 16.8 us -> none  [the longest x6 7.33 us: local(): prod = jnp.dot(prod, iterate_full, precision=hp)]
    transpose x5 -> x0, local copies, waits for them, and re-layouts: 14.3 us -> none  [the longest x3 9.2 us: gather_axes(): parts = jnp.swapaxes(from_everyone(initial, near), 0, 1)]
  transfers between devices with their start and end apart: 8 -> 0, of which waited for: 8 -> 0; matrix products, arithmetic and copies ran while one was open for 1% -> 0% of each run, Pallas kernels for 0% -> 0%
where the time goes in v1:
time: 133 us; the launch traced here: 132 us
  blocking collectives  108 us (81%)
  Pallas kernels  23.3 us (18%)
    all_to_all x2, blocking collectives, exchange(): return lax.all_to_all(x, AXES, 0, 0, tiled=True).reshape(rows, LANES)  108 us
    pallas_call x1, Pallas kernels, local(): pl.pallas_call(functools.partial(whiten_kernel, rows_total), out_shape=(j...  17.9 us
    pallas_call x1, Pallas kernels, local(): pl.pallas_call(gram_kernel, out_shape=packed_type, in_specs=[vmem], out_s...  2.86 us

profile of v1, /device:TPU:1, one launch (start us, length us, event | category | flops | bytes accessed | tf_op | source)
XLA Modules:
  0.0 132.0 jit_solution(6270369792688574377)
XLA Ops:
  0.6 2.9 %gram.1 = f32[2560,128]{1,0:T(8,128)} custom-call(bf16[512,768]{1,0:T(8,128)(2,1)} %e_ref.3), custom_call_target="tpu_custom_call" | custom-call | tf_op jit(solution)/shard_map/gram/pallas_call | solution.py:212
  3.5 59.7 %all_to_all.10 = f32[512,1,640]{2,1,0:T(1,128)} all-to-all(f32[512,1,640]{2,1,0:T(1,128)} %bitcast.8), channel_id=1, replica_groups=mesh['grp'=8,'row_0'=8,'row_1'=4,'row_2'=2] {'grp','row_0','row_1','row_2'}, dimensions={0} | all-to-all | bytes 2621440 | tf_op jit(solution)/shard_map/all_to_all | solution.py:210
  63.1 2.6 %total.1 = f32[2560,128]{1,0:T(8,128)} custom-call(f32[2560,128]{1,0:T(8,128)} %bitcast.6), custom_call_target="tpu_custom_call" | custom-call | tf_op jit(solution)/shard_map/total/pallas_call | solution.py:213
  65.7 48.3 %all_to_all.11 = f32[512,1,640]{2,1,0:T(1,128)} all-to-all(f32[512,1,640]{2,1,0:T(1,128)} %bitcast.7), channel_id=1, replica_groups=mesh['grp'=8,'row_0'=8,'row_1'=4,'row_2'=2] {'grp','row_0','row_1','row_2'}, dimensions={0} | all-to-all | bytes 2621440 | tf_op jit(solution)/shard_map/all_to_all | solution.py:210
  114.1 17.9 %whiten.1 = (bf16[512,768]{1,0:T(8,128)(2,1)}, f32[1,1]{1,0:T(1,128)}) custom-call(bf16[512,768]{1,0:T(8,128)(2,1)} %e_ref.3, f32[2560,128]{1,0:T(8,128)} %bitcast.5), custom_call_target="tpu_custom_call" | custom-call | tf_op jit(solution)/shard_map/whiten/pallas_call | solution.py:218

commit v2 on v1

--- a/solution.py
+++ b/solution.py
@@ -18,17 +18,16 @@
 
 def layout(width):
     nb = width // LANES
-    off = {}
-    at = 0
+    place = {}
+    at = [0, 0]
     for i in range(nb):
-        for j in range(i + 1, nb):
-            off[i, j] = at
-            at += LANES
-    merged = {}
-    for i in range(0, nb, 2):
-        merged[i] = at
-        at += LANES
-    return nb, off, merged, at
+        half = 0 if i < TILE // LANES else 1
+        for j in range(i, nb):
+            if j == i and i % 2:
+                continue
+            place[i, j] = (half, at[half])
+            at[half] += LANES
+    return nb, place, at[1], max(at[0], at[1] + 16)
 
 
 def upper(shape):
@@ -37,35 +36,50 @@
     return r <= c, r == c
 
 
-def gram_kernel(e_ref, o_ref):
+def gram_kernel(e_ref, *refs):
+    o_ref = refs[-1]
     width = e_ref.shape[1]
-    nb, off, merged, tail = layout(width)
-    e = e_ref[...]
-    keep, diag = upper((LANES, LANES))
-    diagonal = {}
-    lines = []
-    for big in range(0, width, TILE):
+    nb, place, tail, _ = layout(width)
+    core = lax.axis_index(AXES[3])
+
+    def put(at, rows):
+        if len(refs) > 1:
+            rows = rows + refs[0][at : at + rows.shape[0], :]
+        o_ref[at : at + rows.shape[0], :] = rows
+
+    def tile_row(big):
+        keep, _ = upper((LANES, LANES))
         g = lax.dot_general(
-            e[:, big : big + TILE], e[:, big:], (((0,), (0,)), ((), ())), preferred_element_type=F32
+            e_ref[:, big : big + TILE], e_ref[:, big:], (((0,), (0,)), ((), ())), preferred_element_type=F32
         )
-        for i in range(big // LANES, (big + TILE) // LANES):
-            r = i * LANES - big
-            for j in range(i, nb):
-                block = g[r : r + LANES, j * LANES - big : (j + 1) * LANES - big]
-                if i == j:
-                    diagonal[i] = block
-                else:
-                    o_ref[off[i, j] : off[i, j] + LANES, :] = block
         i = big // LANES
-        a, b = diagonal[i], diagonal[i + 1]
-        o_ref[merged[i] : merged[i] + LANES, :] = jnp.where(keep, a, b)
-        lines.append(jnp.sum(jnp.where(diag, b, 0.0), axis=0, keepdims=True))
-    colsum = jnp.sum(e.astype(F32), axis=0, keepdims=True)
-    o_ref[tail:, :] = jnp.zeros((o_ref.shape[0] - tail, LANES), F32)
-    for k in range(nb):
-        o_ref[tail + k : tail + k + 1, :] = colsum[:, k * LANES : (k + 1) * LANES]
-    for k, line in enumerate(lines):
-        o_ref[tail + nb + k : tail + nb + k + 1, :] = line
+
+        def block(r, j):
+            return g[r * LANES : (r + 1) * LANES, j * LANES - big : (j + 1) * LANES - big]
+
+        put(place[i, i][1], jnp.where(keep, block(0, i), block(1, i + 1)))
+        for r in range(2):
+            for j in range(i + r + 1, nb):
+                put(place[i + r, j][1], block(r, j))
+
+    @pl.when(core == 0)
+    def _():
+        tile_row(0)
+
+    @pl.when(core == 1)
+    def _():
+        for big in range(TILE, width, TILE):
+            tile_row(big)
+        e = e_ref[...].astype(F32)
+        colsum = jnp.sum(e, axis=0, keepdims=True)
+        lines = [colsum[:, k * LANES : (k + 1) * LANES] for k in range(nb)]
+        for k in range(1, nb, 2):
+            x = e[:, k * LANES : (k + 1) * LANES]
+            lines.append(jnp.sum(x * x, axis=0, keepdims=True))
+        used = tail + len(lines)
+        for k, line in enumerate(lines):
+            put(tail + k, line)
+        o_ref[used:, :] = jnp.zeros((o_ref.shape[0] - used, LANES), F32)
 
 
 def total_kernel(piece, x_ref, o_ref):
@@ -84,28 +98,38 @@
     return hi, lo
 
 
-def whiten_kernel(rows_total, e_ref, p_ref, o_ref, en_ref, s_ref, r_ref, q_ref, sh, sl, ah, al, bh, bl, w_ref):
+def whiten_kernel(rows_total, e_ref, own_ref, other_ref, o_ref, en_ref, half_ref, s_ref, r_ref, q_ref, sh, sl, ah, al, bh, bl, w_ref):
     rows_dev, width = e_ref.shape
-    nb, off, merged, tail = layout(width)
+    nb, place, tail, _ = layout(width)
     inv = 1.0 / rows_total
     keep, diag = upper((LANES, LANES))
-    means = [p_ref[tail + k : tail + k + 1, :] * inv for k in range(nb)]
+    core = lax.axis_index(AXES[3])
+    half_ref[core] = own_ref[...]
+    half_ref[1 - core] = other_ref[...]
+
+    def packed(i, j):
+        half, at = place[i, j]
+        return half_ref[half, at : at + LANES, :]
+
+    def line(k):
+        return half_ref[1, tail + k : tail + k + 1, :]
+
+    means = [line(k) * inv for k in range(nb)]
     down = [jnp.transpose(jnp.broadcast_to(m, (LANES, LANES))) for m in means]
 
     squares = jnp.zeros((LANES, LANES), F32)
     for i in range(nb):
         for j in range(i, nb):
             if i != j:
-                block = p_ref[off[i, j] : off[i, j] + LANES, :]
+                block = packed(i, j)
             else:
                 base = i - i % 2
-                packed = p_ref[merged[base] : merged[base] + LANES, :]
-                mirror = jnp.transpose(packed)
+                both = packed(base, base)
+                mirror = jnp.transpose(both)
                 if i == base:
-                    block = jnp.where(keep, packed, mirror)
+                    block = jnp.where(keep, both, mirror)
                 else:
-                    line = p_ref[tail + nb + base // 2 : tail + nb + base // 2 + 1, :]
-                    block = jnp.where(diag, line, jnp.where(keep, mirror, packed))
+                    block = jnp.where(diag, line(nb + base // 2), jnp.where(keep, mirror, both))
             cov = block * inv - down[i] * means[j]
             squares = squares + (cov * cov) * (1.0 if i == j else 2.0)
             s_ref[i * LANES : (i + 1) * LANES, j * LANES : (j + 1) * LANES] = cov
@@ -197,32 +221,54 @@
 
 def local(embeddings):
     rows_dev, width = embeddings.shape
-    peers = lax.axis_size(AXES)
-    rows_total = rows_dev * peers
-    _, _, _, tail = layout(width)
-    piece = -(-(tail + 16) // peers)
-    rows = piece * peers
-    packed_type = jax.ShapeDtypeStruct((rows, LANES), F32)
+    rows_total = rows_dev * lax.axis_size(AXES)
+    chips = lax.axis_size(AXES[:3])
+    _, _, _, need = layout(width)
+    piece = -(-need // chips)
+    rows = piece * chips
+    half_type = jax.ShapeDtypeStruct((rows, LANES), F32)
     vmem = pl.BlockSpec(memory_space=pltpu.VMEM)
 
     def exchange(x):
-        x = x.reshape(peers, 1, piece * LANES)
-        return lax.all_to_all(x, AXES, 0, 0, tiled=True).reshape(rows, LANES)
-
-    packed = pl.pallas_call(gram_kernel, out_shape=packed_type, in_specs=[vmem], out_specs=vmem, name="gram")(embeddings)
-    summed = pl.pallas_call(
-        functools.partial(total_kernel, piece), out_shape=packed_type, in_specs=[vmem], out_specs=vmem, name="total"
-    )(exchange(packed))
-    everything = exchange(summed)
+        x = x.reshape(chips, 1, piece * LANES)
+        return lax.all_to_all(x, AXES[:3], 0, 0, tiled=True).reshape(rows, LANES)
+
+    def swap(x):
+        return lax.ppermute(x, AXES[3], [(0, 1), (1, 0)])
+
+    def call(kernel, out, name, *args, flops=0, mib=8, **rest):
+        cost = pl.CostEstimate(flops=flops, bytes_accessed=0, transcendentals=0)
+        return pl.pallas_call(
+            kernel,
+            out_shape=out,
+            in_specs=[vmem] * len(args),
+            out_specs=jax.tree.map(lambda _: vmem, out),
+            cost_estimate=cost,
+            compiler_params=pltpu.CompilerParams(vmem_limit_bytes=mib << 20),
+            name=name,
+            **rest,
+        )(*args)
+
+    flops = 2 * rows_dev * width * TILE
+    theirs = swap(embeddings)
+    own = call(gram_kernel, half_type, "gram_own", embeddings, flops=flops)
+    packed = call(gram_kernel, half_type, "gram_both", theirs, own, flops=flops)
+    summed = call(functools.partial(total_kernel, piece), half_type, "total", exchange(packed))
+    half = exchange(summed)
     square = (width, width)
-    whitened, energy = pl.pallas_call(
+    whitened, energy = call(
         functools.partial(whiten_kernel, rows_total),
-        out_shape=(jax.ShapeDtypeStruct((rows_dev, width), BF16), jax.ShapeDtypeStruct((1, 1), F32)),
-        in_specs=[vmem, vmem],
-        out_specs=(vmem, vmem),
-        scratch_shapes=[pltpu.VMEM(square, F32)] * 3 + [pltpu.VMEM(square, BF16)] * 7,
-        name="whiten",
-    )(embeddings, everything)
+        (jax.ShapeDtypeStruct((rows_dev, width), BF16), jax.ShapeDtypeStruct((1, 1), F32)),
+        "whiten",
+        embeddings,
+        half,
+        swap(half),
+        flops=40 * width**3,
+        mib=32,
+        scratch_shapes=[pltpu.VMEM((2, rows, LANES), F32)]
+        + [pltpu.VMEM(square, F32)] * 3
+        + [pltpu.VMEM(square, BF16)] * 7,
+    )
     return whitened, energy.reshape(())
 
 

time: 133 us -> 104 us (0.78)
  blocking collectives: 108 us -> 67.1 us
  starting transfers between devices: 0 us -> 14.8 us
  Pallas kernels: 23.3 us -> 17.6 us
  waiting for transfers between devices: 0 us -> 1.97 us
    all_to_all x2, blocking collectives: 108 us -> 67.1 us  [exchange(): return lax.all_to_all(x, AXES[:3], 0, 0, tiled=True).reshape(rows, LANES)]
    ppermute x0 -> x2, starting transfers between devices: none -> 14.8 us  [swap(): return lax.ppermute(x, AXES[3], [(0, 1), (1, 0)])]
    pallas_call x3 -> x4, Pallas kernels: 23.3 us -> 17.6 us  [call(): pl.pallas_call(kernel, out_shape=out, in_specs=[vmem] * len(args), out_sp...]
    ppermute x0 -> x2, waiting for transfers between devices: none -> 1.97 us  [swap(): return lax.ppermute(x, AXES[3], [(0, 1), (1, 0)])]
  transfers between devices with their start and end apart: 0 -> 2, of which waited for: 0 -> 2; matrix products, arithmetic and copies ran while one was open for 0% -> 0% of each run, Pallas kernels for 0% -> 0%
where the time goes in v2:
time: 104 us; the launch traced here: 103 us
  blocking collectives  67.1 us (65%)
  Pallas kernels  17.6 us (17%)
  starting transfers between devices  14.8 us (14%)
  waiting for transfers between devices  1.97 us (2%)
  local copies, waits for them, and re-layouts  1.13 us (1%)
    all_to_all x2, blocking collectives, exchange(): return lax.all_to_all(x, AXES[:3], 0, 0, tiled=True).reshape(rows, LANES)  67.1 us
    pallas_call x4, Pallas kernels, call(): pl.pallas_call(kernel, out_shape=out, in_specs=[vmem] * len(args), out_sp...  17.6 us
    ppermute x2, starting transfers between devices, swap(): return lax.ppermute(x, AXES[3], [(0, 1), (1, 0)])  14.8 us
  transfers between devices with their start and end apart: 2, of which 2 were waited for; matrix products, arithmetic and copies ran while one was open for 0% of the time, Pallas kernels for 0%

profile of v2, /device:TPU:1, one launch (start us, length us, event | category | flops | bytes accessed | tf_op | source)
XLA Modules:
  0.0 103.3 jit_solution(10684093587692131035)
XLA Ops:
  0.6 8.7 %collective-permute-start = (bf16[512,768]{1,0:T(8,128)(2,1)}, bf16[512,768]{1,0:T(8,128)(2,1)S(1)}, u32[]{:S(2)}, u32[]{:S(2)}) collective-permute-start(bf16[512,768]{1,0:T(8,128)(2,1)} %e_ref.3), channel_id=1, source_target_pairs={{0,1},{1,0},{2,3},{3,2},{4,5},{5,4},{6,7},{7,6},{8,9},{9,8},{10,11... | collective-permute-start | bytes 2359304 | tf_op jit(solution)/shard_map/ppermute | solution.py:237
  9.4 0.0 copy-start
  9.4 1.1 %copy-done = bf16[512,768]{1,0:T(8,128)(2,1)S(1)} copy-done((bf16[512,768]{1,0:T(8,128)(2,1)S(1)}, bf16[512,768]{1,0:T(8,128)(2,1)}, u32[]{:S(2)}) %copy-start) | copy-done | bytes 786456
  10.5 0.5 gram_own.1.refs_0_
  11.0 0.5 collective-permute-done.e_ref
  11.5 0.5 gram_both.1
  12.0 37.2 %all_to_all.10 = f32[256,1,640]{2,1,0:T(1,128)S(1)} all-to-all(f32[256,1,640]{2,1,0:T(1,128)S(1)} %bitcast.5), channel_id=1, replica_groups=mesh['grp'=8,'row_0'=8,'row_1'=4,'row_2'=2] {'grp','row_0','row_1'}, dimensions={0} | all-to-all | bytes 1310720 | tf_op jit(solution)/shard_map/all_to_all | solution.py:234
  49.2 0.1 total.1
  49.3 0.0 copy-start.1
  49.3 29.9 %all_to_all.11 = f32[256,1,640]{2,1,0:T(1,128)S(1)} all-to-all(f32[256,1,640]{2,1,0:T(1,128)S(1)} %bitcast.7), channel_id=1, replica_groups=mesh['grp'=8,'row_0'=8,'row_1'=4,'row_2'=2] {'grp','row_0','row_1'}, dimensions={0} | all-to-all | bytes 1310720 | tf_op jit(solution)/shard_map/all_to_all | solution.py:234
  79.2 6.0 %collective-permute-start.1 = (f32[1280,128]{1,0:T(8,128)S(1)}, f32[1280,128]{1,0:T(8,128)S(1)}, u32[]{:S(2)}, u32[]{:S(2)}) collective-permute-start(f32[1280,128]{1,0:T(8,128)S(1)} %bitcast.8), channel_id=1, source_target_pairs={{0,1},{1,0},{2,3},{3,2},{4,5},{5,4},{6,7},{7,6},{8,9},{9,8},{10,11... | collective-permute-start | bytes 1966088 | tf_op jit(solution)/shard_map/ppermute | solution.py:237
  85.3 1.5 %collective-permute-done.1.other_ref = f32[1280,128]{1,0:T(8,128)S(1)} collective-permute-done((f32[1280,128]{1,0:T(8,128)S(1)}, f32[1280,128]{1,0:T(8,128)S(1)}, u32[]{:S(2)}, u32[]{:S(2)}) %collective-permute-start.1) | collective-permute-done | bytes 655392 | tf_op jit(solution)/shard_map/ppermute | solution.py:237
  86.8 0.0 copy-done.1
  86.8 16.5 %whiten.1 = (bf16[512,768]{1,0:T(8,128)(2,1)}, f32[1,1]{1,0:T(1,128)}) custom-call(bf16[512,768]{1,0:T(8,128)(2,1)S(1)} %copy-done.1, f32[1280,128]{1,0:T(8,128)S(1)} %bitcast.9, f32[1280,128]{1,0:T(8,128)S(1)} %collective-permute-done.1.other_ref), custom_call_target="tpu_custom_call" | custom-call | flops 18119393280 | tf_op jit(solution)/shard_map/whiten/pallas_call | solution.py:241
Async XLA Ops:
  0.6 10.9 %collective-permute-start = (bf16[512,768]{1,0:T(8,128)(2,1)}, bf16[512,768]{1,0:T(8,128)(2,1)S(1)}, u32[]{:S(2)}, u32[]{:S(2)}) collective-permute-start(bf16[512,768]{1,0:T(8,128)(2,1)} %e_ref.3), channel_id=1, source_target_pairs={{0,1},{1,0},{2,3},{3,2},{4,5},{5,4},{6,7},{7,6},{8,9},{9,8},{10,11... | collective-permute-start | bytes 2359304 | tf_op jit(solution)/shard_map/ppermute | solution.py:237
  9.4 1.1 %copy-start = (bf16[512,768]{1,0:T(8,128)(2,1)S(1)}, bf16[512,768]{1,0:T(8,128)(2,1)}, u32[]{:S(2)}) copy-start(bf16[512,768]{1,0:T(8,128)(2,1)} %e_ref.3) | copy-start | bytes 2359300
  49.3 37.5 %copy-start.1 = (bf16[512,768]{1,0:T(8,128)(2,1)S(1)}, bf16[512,768]{1,0:T(8,128)(2,1)}, u32[]{:S(2)}) copy-start(bf16[512,768]{1,0:T(8,128)(2,1)} %e_ref.3) | copy-start | bytes 2359300
  79.2 7.6 %collective-permute-start.1 = (f32[1280,128]{1,0:T(8,128)S(1)}, f32[1280,128]{1,0:T(8,128)S(1)}, u32[]{:S(2)}, u32[]{:S(2)}) collective-permute-start(f32[1280,128]{1,0:T(8,128)S(1)} %bitcast.8), channel_id=1, source_target_pairs={{0,1},{1,0},{2,3},{3,2},{4,5},{5,4},{6,7},{7,6},{8,9},{9,8},{10,11... | collective-permute-start | bytes 1966088 | tf_op jit(solution)/shard_map/ppermute | solution.py:237

commit v3 on v2

--- a/solution.py
+++ b/solution.py
@@ -82,14 +82,13 @@
         o_ref[used:, :] = jnp.zeros((o_ref.shape[0] - used, LANES), F32)
 
 
-def total_kernel(piece, x_ref, o_ref):
-    period = 8 * piece
-    groups = x_ref.shape[0] // period
-    acc = jnp.sum(x_ref[...].reshape(groups, period, LANES), axis=0)
-    for shift in (piece, 2 * piece, 4 * piece):
-        acc = acc + jnp.concatenate([acc[period - shift :], acc[: period - shift]], axis=0)
-    for g in range(groups):
-        o_ref[g * period : (g + 1) * period, :] = acc
+def total_kernel(peers, copies, x_ref, o_ref):
+    rows = x_ref.shape[0] // peers
+    acc = x_ref[:rows, :]
+    for n in range(1, peers):
+        acc = acc + x_ref[n * rows : (n + 1) * rows, :]
+    for n in range(copies):
+        o_ref[n * rows : (n + 1) * rows, :] = acc
 
 
 def split(x):
@@ -222,16 +221,16 @@
 def local(embeddings):
     rows_dev, width = embeddings.shape
     rows_total = rows_dev * lax.axis_size(AXES)
-    chips = lax.axis_size(AXES[:3])
+    sizes = [lax.axis_size(axis) for axis in AXES]
     _, _, _, need = layout(width)
-    piece = -(-need // chips)
-    rows = piece * chips
+    unit = 8 * sizes[0] * sizes[2]
+    rows = -(-need // unit) * unit
     half_type = jax.ShapeDtypeStruct((rows, LANES), F32)
     vmem = pl.BlockSpec(memory_space=pltpu.VMEM)
 
-    def exchange(x):
-        x = x.reshape(chips, 1, piece * LANES)
-        return lax.all_to_all(x, AXES[:3], 0, 0, tiled=True).reshape(rows, LANES)
+    def exchange(x, n):
+        y = x.reshape(sizes[n], 1, x.shape[0] * LANES // sizes[n])
+        return lax.all_to_all(y, AXES[n], 0, 0, tiled=True).reshape(x.shape)
 
     def swap(x):
         return lax.ppermute(x, AXES[3], [(0, 1), (1, 0)])
@@ -253,8 +252,16 @@
     theirs = swap(embeddings)
     own = call(gram_kernel, half_type, "gram_own", embeddings, flops=flops)
     packed = call(gram_kernel, half_type, "gram_both", theirs, own, flops=flops)
-    summed = call(functools.partial(total_kernel, piece), half_type, "total", exchange(packed))
-    half = exchange(summed)
+
+    def total(x, peers, copies):
+        out = jax.ShapeDtypeStruct((x.shape[0] // peers * copies, LANES), F32)
+        return call(functools.partial(total_kernel, peers, copies), out, f"total_{peers}_{copies}", x)
+
+    x = total(exchange(packed, 2), sizes[2], 1)
+    x = total(exchange(x, 0), sizes[0], sizes[1])
+    x = total(exchange(x, 1), sizes[1], sizes[0])
+    x = total(exchange(x, 0), 1, sizes[2])
+    half = exchange(x, 2)
     square = (width, width)
     whitened, energy = call(
         functools.partial(whiten_kernel, rows_total),

time: 104 us -> 102 us (0.981)
  blocking collectives: 67.1 us -> 62.8 us
  starting transfers between devices: 14.8 us -> 17.3 us
    all_to_all x2 -> x5, blocking collectives: 67.1 us -> 62.8 us  [exchange(): return lax.all_to_all(y, AXES[n], 0, 0, tiled=True).reshape(x.shape)]
    ppermute x2, starting transfers between devices: 14.8 us -> 17.3 us  [swap(): return lax.ppermute(x, AXES[3], [(0, 1), (1, 0)])]
    pallas_call x4 -> x7, Pallas kernels: 17.6 us -> 17.6 us  [call(): pl.pallas_call(kernel, out_shape=out, in_specs=[vmem] * len(args), out_sp...]
  transfers between devices with their start and end apart: 2 -> 2, of which waited for: 2 -> 2; matrix products, arithmetic and copies ran while one was open for 0% -> 0% of each run, Pallas kernels for 0% -> 1%
where the time goes in v3:
time: 102 us
  blocking collectives  62.8 us (62%)
  Pallas kernels  17.6 us (17%)
  starting transfers between devices  17.3 us (17%)
  waiting for transfers between devices  1.97 us (2%)
  local copies, waits for them, and re-layouts  1.13 us (1%)
    all_to_all x5, blocking collectives, exchange(): return lax.all_to_all(y, AXES[n], 0, 0, tiled=True).reshape(x.shape)  62.8 us
    pallas_call x7, Pallas kernels, call(): pl.pallas_call(kernel, out_shape=out, in_specs=[vmem] * len(args), out_sp...  17.6 us
    ppermute x2, starting transfers between devices, swap(): return lax.ppermute(x, AXES[3], [(0, 1), (1, 0)])  17.3 us
  transfers between devices with their start and end apart: 2, of which 2 were waited for; matrix products, arithmetic and copies ran while one was open for 0% of the time, Pallas kernels for 1%

profile of v3, /device:TPU:1, one launch (start us, length us, event | category | flops | bytes accessed | tf_op | source)
XLA Modules:
  0.0 101.6 jit_solution(11190916932504546289)
XLA Ops:
  0.6 8.7 %collective-permute-start = (bf16[512,768]{1,0:T(8,128)(2,1)}, bf16[512,768]{1,0:T(8,128)(2,1)S(1)}, u32[]{:S(2)}, u32[]{:S(2)}) collective-permute-start(bf16[512,768]{1,0:T(8,128)(2,1)} %e_ref.3), channel_id=1, source_target_pairs={{0,1},{1,0},{2,3},{3,2},{4,5},{5,4},{6,7},{7,6},{8,9},{9,8},{10,11... | collective-permute-start | bytes 2359304 | tf_op jit(solution)/shard_map/ppermute | solution.py:236
  9.4 0.0 copy-start
  9.4 1.1 %copy-done = bf16[512,768]{1,0:T(8,128)(2,1)S(1)} copy-done((bf16[512,768]{1,0:T(8,128)(2,1)S(1)}, bf16[512,768]{1,0:T(8,128)(2,1)}, u32[]{:S(2)}) %copy-start) | copy-done | bytes 786456
  10.5 0.5 gram_own.1.refs_0_
  11.0 0.5 collective-permute-done.e_ref
  11.5 0.5 gram_both.1
  12.0 13.1 %all_to_all.25 = f32[4,1,40960]{2,1,0:T(1,128)S(1)} all-to-all(f32[4,1,40960]{2,1,0:T(1,128)S(1)} %bitcast.11), channel_id=1, replica_groups=mesh['grp'=8,'row_0'=8,'row_1'=4,'row_2'=2] {'row_1'}, dimensions={0} | all-to-all | bytes 1310720 | tf_op jit(solution)/shard_map/all_to_all | solution.py:233
  25.2 10.8 %all_to_all.26 = f32[8,1,5120]{2,1,0:T(1,128)S(1)} all-to-all(f32[8,1,5120]{2,1,0:T(1,128)S(1)} %bitcast.20), channel_id=1, replica_groups=mesh['grp'=8,'row_0'=8,'row_1'=4,'row_2'=2] {'grp'}, dimensions={0} | all-to-all | bytes 327680 | tf_op jit(solution)/shard_map/all_to_all | solution.py:233
  36.0 18.1 %all_to_all.27 = f32[8,1,5120]{2,1,0:T(1,128)S(1)} all-to-all(f32[8,1,5120]{2,1,0:T(1,128)S(1)} %bitcast.17), channel_id=1, replica_groups=mesh['grp'=8,'row_0'=8,'row_1'=4,'row_2'=2] {'row_0'}, dimensions={0} | all-to-all | bytes 327680 | tf_op jit(solution)/shard_map/all_to_all | solution.py:233
  54.1 10.7 %all_to_all.28 = f32[8,1,5120]{2,1,0:T(1,128)S(1)} all-to-all(f32[8,1,5120]{2,1,0:T(1,128)S(1)} %bitcast.19), channel_id=1, replica_groups=mesh['grp'=8,'row_0'=8,'row_1'=4,'row_2'=2] {'grp'}, dimensions={0} | all-to-all | bytes 327680 | tf_op jit(solution)/shard_map/all_to_all | solution.py:233
  64.8 0.0 copy-start.1
  64.8 10.2 %all_to_all.29 = f32[4,1,40960]{2,1,0:T(1,128)S(1)} all-to-all(f32[4,1,40960]{2,1,0:T(1,128)S(1)} %bitcast.13), channel_id=1, replica_groups=mesh['grp'=8,'row_0'=8,'row_1'=4,'row_2'=2] {'row_1'}, dimensions={0} | all-to-all | bytes 1310720 | tf_op jit(solution)/shard_map/all_to_all | solution.py:233
  75.0 8.6 %collective-permute-start.1 = (f32[1280,128]{1,0:T(8,128)S(1)}, f32[1280,128]{1,0:T(8,128)S(1)}, u32[]{:S(2)}, u32[]{:S(2)}) collective-permute-start(f32[1280,128]{1,0:T(8,128)S(1)} %bitcast.14), channel_id=1, source_target_pairs={{0,1},{1,0},{2,3},{3,2},{4,5},{5,4},{6,7},{7,6},{8,9},{9,8},{10,11... | collective-permute-start | bytes 1966088 | tf_op jit(solution)/shard_map/ppermute | solution.py:236
  83.6 1.5 %collective-permute-done.1.other_ref = f32[1280,128]{1,0:T(8,128)S(1)} collective-permute-done((f32[1280,128]{1,0:T(8,128)S(1)}, f32[1280,128]{1,0:T(8,128)S(1)}, u32[]{:S(2)}, u32[]{:S(2)}) %collective-permute-start.1) | collective-permute-done | bytes 655392 | tf_op jit(solution)/shard_map/ppermute | solution.py:236
  85.1 0.0 copy-done.1
  85.1 16.5 %whiten.1 = (bf16[512,768]{1,0:T(8,128)(2,1)}, f32[1,1]{1,0:T(1,128)}) custom-call(bf16[512,768]{1,0:T(8,128)(2,1)S(1)} %copy-done.1, f32[1280,128]{1,0:T(8,128)S(1)} %bitcast.15, f32[1280,128]{1,0:T(8,128)S(1)} %collective-permute-done.1.other_ref), custom_call_target="tpu_custom_call" | custom-call | flops 18119393280 | tf_op jit(solution)/shard_map/whiten/pallas_call | solution.py:240
  (4 shorter events, 0.1 us)
Async XLA Ops:
  0.6 10.9 %collective-permute-start = (bf16[512,768]{1,0:T(8,128)(2,1)}, bf16[512,768]{1,0:T(8,128)(2,1)S(1)}, u32[]{:S(2)}, u32[]{:S(2)}) collective-permute-start(bf16[512,768]{1,0:T(8,128)(2,1)} %e_ref.3), channel_id=1, source_target_pairs={{0,1},{1,0},{2,3},{3,2},{4,5},{5,4},{6,7},{7,6},{8,9},{9,8},{10,11... | collective-permute-start | bytes 2359304 | tf_op jit(solution)/shard_map/ppermute | solution.py:236
  9.4 1.1 %copy-start = (bf16[512,768]{1,0:T(8,128)(2,1)S(1)}, bf16[512,768]{1,0:T(8,128)(2,1)}, u32[]{:S(2)}) copy-start(bf16[512,768]{1,0:T(8,128)(2,1)} %e_ref.3) | copy-start | bytes 2359300
  64.8 20.3 %copy-start.1 = (bf16[512,768]{1,0:T(8,128)(2,1)S(1)}, bf16[512,768]{1,0:T(8,128)(2,1)}, u32[]{:S(2)}) copy-start(bf16[512,768]{1,0:T(8,128)(2,1)} %e_ref.3) | copy-start | bytes 2359300
  75.0 10.1 %collective-permute-start.1 = (f32[1280,128]{1,0:T(8,128)S(1)}, f32[1280,128]{1,0:T(8,128)S(1)}, u32[]{:S(2)}, u32[]{:S(2)}) collective-permute-start(f32[1280,128]{1,0:T(8,128)S(1)} %bitcast.14), channel_id=1, source_target_pairs={{0,1},{1,0},{2,3},{3,2},{4,5},{5,4},{6,7},{7,6},{8,9},{9,8},{10,11... | collective-permute-start | bytes 1966088 | tf_op jit(solution)/shard_map/ppermute | solution.py:236

commit v4 on v3

--- a/solution.py
+++ b/solution.py
@@ -10,6 +10,7 @@
 
 ITERS = 4
 AXES = ("grp", "row_0", "row_1", "row_2")
+PLANE = ("grp", "row_1")
 LANES = 128
 TILE = 256
 F32 = jnp.float32
@@ -161,6 +162,13 @@
         a, b = span(i), span(j)
         return dot(xh[a, :], yh[:, b]) + (dot(xh[a, :], yl[:, b]) + dot(xl[a, :], yh[:, b]))
 
+    def squared(xh, xl, i, j):
+        if i != j:
+            return product(xh, xl, xh, xl, i, j)
+        a = span(i)
+        cross = dot(xh[a, :], xl[:, a])
+        return dot(xh[a, :], xh[:, a]) + (cross + jnp.transpose(cross))
+
     def put(h_ref, l_ref, i, j, x):
         h_ref[span(i), span(j)], l_ref[span(i), span(j)] = split(x)
         if i != j:
@@ -169,7 +177,7 @@
     def double_step(t_ref, th, tl, x_ref):
         for i, j in pairs:
             at = (span(i), span(j))
-            t2 = product(th, tl, th, tl, i, j)
+            t2 = squared(th, tl, i, j)
             t = t_ref[at]
             put(ah, al, i, j, t2)
             put(bh, bl, i, j, 0.0625 * t2 - 0.5625 * t)
@@ -183,7 +191,7 @@
         put(ah, al, i, j, r_ref[span(i), span(j)])
     for i, j in pairs:
         at = (span(i), span(j))
-        put(bh, bl, i, j, 4.5 * r_ref[at] + product(ah, al, ah, al, i, j))
+        put(bh, bl, i, j, 4.5 * r_ref[at] + squared(ah, al, i, j))
     for i, j in pairs:
         at = (span(i), span(j))
         q_ref[at] = 5.0625 * s_ref[at] + product(sh, sl, bh, bl, i, j)
@@ -223,14 +231,16 @@
     rows_total = rows_dev * lax.axis_size(AXES)
     sizes = [lax.axis_size(axis) for axis in AXES]
     _, _, _, need = layout(width)
-    unit = 8 * sizes[0] * sizes[2]
+    plane = lax.axis_size(PLANE)
+    unit = 8 * plane
     rows = -(-need // unit) * unit
     half_type = jax.ShapeDtypeStruct((rows, LANES), F32)
     vmem = pl.BlockSpec(memory_space=pltpu.VMEM)
 
-    def exchange(x, n):
-        y = x.reshape(sizes[n], 1, x.shape[0] * LANES // sizes[n])
-        return lax.all_to_all(y, AXES[n], 0, 0, tiled=True).reshape(x.shape)
+    def exchange(x, axes):
+        peers = lax.axis_size(axes)
+        y = x.reshape(peers, 1, x.shape[0] * LANES // peers)
+        return lax.all_to_all(y, axes, 0, 0, tiled=True).reshape(x.shape)
 
     def swap(x):
         return lax.ppermute(x, AXES[3], [(0, 1), (1, 0)])
@@ -257,11 +267,9 @@
         out = jax.ShapeDtypeStruct((x.shape[0] // peers * copies, LANES), F32)
         return call(functools.partial(total_kernel, peers, copies), out, f"total_{peers}_{copies}", x)
 
-    x = total(exchange(packed, 2), sizes[2], 1)
-    x = total(exchange(x, 0), sizes[0], sizes[1])
-    x = total(exchange(x, 1), sizes[1], sizes[0])
-    x = total(exchange(x, 0), 1, sizes[2])
-    half = exchange(x, 2)
+    x = total(exchange(packed, PLANE), plane, sizes[1])
+    x = total(exchange(x, AXES[1]), sizes[1], plane)
+    half = exchange(x, PLANE)
     square = (width, width)
     whitened, energy = call(
         functools.partial(whiten_kernel, rows_total),

time: 102 us -> 100 us (0.980)
  starting transfers between devices: 17.3 us -> 15.8 us
    ppermute x2, starting transfers between devices: 17.3 us -> 15.8 us  [swap(): return lax.ppermute(x, AXES[3], [(0, 1), (1, 0)])]
    pallas_call x7 -> x5, Pallas kernels: 17.6 us -> 16.9 us  [call(): pl.pallas_call(kernel, out_shape=out, in_specs=[vmem] * len(args), out_sp...]
    all_to_all x5 -> x3, blocking collectives: 62.8 us -> 63.3 us  [exchange(): return lax.all_to_all(y, axes, 0, 0, tiled=True).reshape(x.shape)]
where the time goes in v4:
time: 100 us; the launch traced here: 99.7 us
  blocking collectives  63.3 us (63%)
  Pallas kernels  16.9 us (17%)
  starting transfers between devices  15.8 us (16%)
  waiting for transfers between devices  1.97 us (2%)
  local copies, waits for them, and re-layouts  1.13 us (1%)
    all_to_all x3, blocking collectives, exchange(): return lax.all_to_all(y, axes, 0, 0, tiled=True).reshape(x.shape)  63.3 us
    pallas_call x5, Pallas kernels, call(): pl.pallas_call(kernel, out_shape=out, in_specs=[vmem] * len(args), out_sp...  16.9 us
    ppermute x2, starting transfers between devices, swap(): return lax.ppermute(x, AXES[3], [(0, 1), (1, 0)])  15.8 us
  transfers between devices with their start and end apart: 2, of which 2 were waited for; matrix products, arithmetic and copies ran while one was open for 0% of the time, Pallas kernels for 1%

profile of v4, /device:TPU:1, one launch (start us, length us, event | category | flops | bytes accessed | tf_op | source)
XLA Modules:
  0.0 99.7 jit_solution(9393153659761238533)
XLA Ops:
  0.6 8.7 %collective-permute-start = (bf16[512,768]{1,0:T(8,128)(2,1)}, bf16[512,768]{1,0:T(8,128)(2,1)S(1)}, u32[]{:S(2)}, u32[]{:S(2)}) collective-permute-start(bf16[512,768]{1,0:T(8,128)(2,1)} %e_ref.3), channel_id=1, source_target_pairs={{0,1},{1,0},{2,3},{3,2},{4,5},{5,4},{6,7},{7,6},{8,9},{9,8},{10,11... | collective-permute-start | bytes 2359304 | tf_op jit(solution)/shard_map/ppermute | solution.py:246
  9.4 0.0 copy-start
  9.4 1.1 %copy-done = bf16[512,768]{1,0:T(8,128)(2,1)S(1)} copy-done((bf16[512,768]{1,0:T(8,128)(2,1)S(1)}, bf16[512,768]{1,0:T(8,128)(2,1)}, u32[]{:S(2)}) %copy-start) | copy-done | bytes 786456
  10.5 0.5 gram_own.1.refs_0_
  11.0 0.5 collective-permute-done.e_ref
  11.5 0.5 gram_both.1
  12.0 23.0 %all_to_all.15 = f32[32,1,5120]{2,1,0:T(1,128)S(1)} all-to-all(f32[32,1,5120]{2,1,0:T(1,128)S(1)} %bitcast.7), channel_id=1, replica_groups=mesh['grp'=8,'row_0'=8,'row_1'=4,'row_2'=2] {'grp','row_1'}, dimensions={0} | all-to-all | bytes 1310720 | tf_op jit(solution)/shard_map/all_to_all | solution.py:243
  35.1 0.1 total_32_8.1
  35.1 18.2 %all_to_all.16 = f32[8,1,5120]{2,1,0:T(1,128)S(1)} all-to-all(f32[8,1,5120]{2,1,0:T(1,128)S(1)} %bitcast.12), channel_id=1, replica_groups=mesh['grp'=8,'row_0'=8,'row_1'=4,'row_2'=2] {'row_0'}, dimensions={0} | all-to-all | bytes 327680 | tf_op jit(solution)/shard_map/all_to_all | solution.py:243
  53.3 0.1 total_8_32.1
  53.4 0.0 copy-start.1
  53.4 22.0 %all_to_all.17 = f32[32,1,5120]{2,1,0:T(1,128)S(1)} all-to-all(f32[32,1,5120]{2,1,0:T(1,128)S(1)} %bitcast.9), channel_id=1, replica_groups=mesh['grp'=8,'row_0'=8,'row_1'=4,'row_2'=2] {'grp','row_1'}, dimensions={0} | all-to-all | bytes 1310720 | tf_op jit(solution)/shard_map/all_to_all | solution.py:243
  75.4 7.0 %collective-permute-start.1 = (f32[1280,128]{1,0:T(8,128)S(1)}, f32[1280,128]{1,0:T(8,128)S(1)}, u32[]{:S(2)}, u32[]{:S(2)}) collective-permute-start(f32[1280,128]{1,0:T(8,128)S(1)} %bitcast.10), channel_id=1, source_target_pairs={{0,1},{1,0},{2,3},{3,2},{4,5},{5,4},{6,7},{7,6},{8,9},{9,8},{10,11... | collective-permute-start | bytes 1966088 | tf_op jit(solution)/shard_map/ppermute | solution.py:246
  82.4 1.5 %collective-permute-done.1.other_ref = f32[1280,128]{1,0:T(8,128)S(1)} collective-permute-done((f32[1280,128]{1,0:T(8,128)S(1)}, f32[1280,128]{1,0:T(8,128)S(1)}, u32[]{:S(2)}, u32[]{:S(2)}) %collective-permute-start.1) | collective-permute-done | bytes 655392 | tf_op jit(solution)/shard_map/ppermute | solution.py:246
  83.9 0.0 copy-done.1
  83.9 15.8 %whiten.1 = (bf16[512,768]{1,0:T(8,128)(2,1)}, f32[1,1]{1,0:T(1,128)}) custom-call(bf16[512,768]{1,0:T(8,128)(2,1)S(1)} %copy-done.1, f32[1280,128]{1,0:T(8,128)S(1)} %bitcast.11, f32[1280,128]{1,0:T(8,128)S(1)} %collective-permute-done.1.other_ref), custom_call_target="tpu_custom_call" | custom-call | flops 18119393280 | tf_op jit(solution)/shard_map/whiten/pallas_call | solution.py:250
Async XLA Ops:
  0.6 10.9 %collective-permute-start = (bf16[512,768]{1,0:T(8,128)(2,1)}, bf16[512,768]{1,0:T(8,128)(2,1)S(1)}, u32[]{:S(2)}, u32[]{:S(2)}) collective-permute-start(bf16[512,768]{1,0:T(8,128)(2,1)} %e_ref.3), channel_id=1, source_target_pairs={{0,1},{1,0},{2,3},{3,2},{4,5},{5,4},{6,7},{7,6},{8,9},{9,8},{10,11... | collective-permute-start | bytes 2359304 | tf_op jit(solution)/shard_map/ppermute | solution.py:246
  9.4 1.1 %copy-start = (bf16[512,768]{1,0:T(8,128)(2,1)S(1)}, bf16[512,768]{1,0:T(8,128)(2,1)}, u32[]{:S(2)}) copy-start(bf16[512,768]{1,0:T(8,128)(2,1)} %e_ref.3) | copy-start | bytes 2359300
  53.4 30.6 %copy-start.1 = (bf16[512,768]{1,0:T(8,128)(2,1)S(1)}, bf16[512,768]{1,0:T(8,128)(2,1)}, u32[]{:S(2)}) copy-start(bf16[512,768]{1,0:T(8,128)(2,1)} %e_ref.3) | copy-start | bytes 2359300
  75.4 8.5 %collective-permute-start.1 = (f32[1280,128]{1,0:T(8,128)S(1)}, f32[1280,128]{1,0:T(8,128)S(1)}, u32[]{:S(2)}, u32[]{:S(2)}) collective-permute-start(f32[1280,128]{1,0:T(8,128)S(1)} %bitcast.10), channel_id=1, source_target_pairs={{0,1},{1,0},{2,3},{3,2},{4,5},{5,4},{6,7},{7,6},{8,9},{9,8},{10,11... | collective-permute-start | bytes 1966088 | tf_op jit(solution)/shard_map/ppermute | solution.py:246

commit v5 on v4

--- a/solution.py
+++ b/solution.py
@@ -10,7 +10,6 @@
 
 ITERS = 4
 AXES = ("grp", "row_0", "row_1", "row_2")
-PLANE = ("grp", "row_1")
 LANES = 128
 TILE = 256
 F32 = jnp.float32
@@ -226,21 +225,36 @@
         o_ref[r : r + TILE, :] = dot(c, w_ref[...]).astype(BF16)
 
 
+def groups(sizes):
+    ny, nz, nx, _ = sizes
+
+    def at(y, z, x, core):
+        return ((y * nz + z) * nx + x) * 2 + core
+
+    planes = [[at(y, z, x, 0) for y in range(ny) for x in range(nx)] for z in range(nz)]
+    planes += [[at(y, z, x, 1) for z in range(nz) for x in range(nx)] for y in range(ny)]
+    lines = [[at(y, z, x, 0) for z in range(nz)] for y in range(ny) for x in range(nx)]
+    lines += [[at(y, z, x, 1) for y in range(ny)] for z in range(nz) for x in range(nx)]
+    return planes, lines
+
+
 def local(embeddings):
     rows_dev, width = embeddings.shape
     rows_total = rows_dev * lax.axis_size(AXES)
     sizes = [lax.axis_size(axis) for axis in AXES]
     _, _, _, need = layout(width)
-    plane = lax.axis_size(PLANE)
-    unit = 8 * plane
-    rows = -(-need // unit) * unit
+    vmem = pl.BlockSpec(memory_space=pltpu.VMEM)
+
+    planes, lines = groups(sizes)
+    plane, line = len(planes[0]), len(lines[0])
+    rows = -(-need // (8 * plane)) * 8 * plane
     half_type = jax.ShapeDtypeStruct((rows, LANES), F32)
-    vmem = pl.BlockSpec(memory_space=pltpu.VMEM)
-
-    def exchange(x, axes):
-        peers = lax.axis_size(axes)
+
+    def exchange(x, members):
+        peers = len(members[0])
         y = x.reshape(peers, 1, x.shape[0] * LANES // peers)
-        return lax.all_to_all(y, axes, 0, 0, tiled=True).reshape(x.shape)
+        out = lax.all_to_all(y, AXES, 0, 0, axis_index_groups=members, tiled=True)
+        return out.reshape(x.shape)
 
     def swap(x):
         return lax.ppermute(x, AXES[3], [(0, 1), (1, 0)])
@@ -267,9 +281,9 @@
         out = jax.ShapeDtypeStruct((x.shape[0] // peers * copies, LANES), F32)
         return call(functools.partial(total_kernel, peers, copies), out, f"total_{peers}_{copies}", x)
 
-    x = total(exchange(packed, PLANE), plane, sizes[1])
-    x = total(exchange(x, AXES[1]), sizes[1], plane)
-    half = exchange(x, PLANE)
+    x = total(exchange(packed, planes), plane, line)
+    x = total(exchange(x, lines), line, plane)
+    half = exchange(x, planes)
     square = (width, width)
     whitened, energy = call(
         functools.partial(whiten_kernel, rows_total),

time: 100 us -> 90.5 us (0.905)
  blocking collectives: 63.3 us -> 54.7 us
  starting transfers between devices: 15.8 us -> 14.8 us
    all_to_all x3, blocking collectives: 63.3 us -> 54.7 us  [exchange(): out = lax.all_to_all(y, AXES, 0, 0, axis_index_groups=members, tiled=True)]
where the time goes in v5:
time: 90.5 us; the launch traced here: 90.2 us
  blocking collectives  54.7 us (60%)
  Pallas kernels  16.9 us (19%)
  starting transfers between devices  14.8 us (16%)
  waiting for transfers between devices  1.97 us (2%)
  local copies, waits for them, and re-layouts  1.13 us (1%)
    all_to_all x3, blocking collectives, exchange(): out = lax.all_to_all(y, AXES, 0, 0, axis_index_groups=members, tiled=True)  54.7 us
    pallas_call x5, Pallas kernels, call(): pl.pallas_call(kernel, out_shape=out, in_specs=[vmem] * len(args), out_sp...  16.9 us
    ppermute x2, starting transfers between devices, swap(): return lax.ppermute(x, AXES[3], [(0, 1), (1, 0)])  14.8 us
    ppermute x2, waiting for transfers between devices, swap(): return lax.ppermute(x, AXES[3], [(0, 1), (1, 0)])  1.97 us
  transfers between devices with their start and end apart: 2, of which 2 were waited for; matrix products, arithmetic and copies ran while one was open for 0% of the time, Pallas kernels for 1%

profile of v5, /device:TPU:1, one launch (start us, length us, event | category | flops | bytes accessed | tf_op | source)
XLA Modules:
  0.0 90.2 jit_solution(17482082137546674746)
XLA Ops:
  0.6 8.7 %collective-permute-start = (bf16[512,768]{1,0:T(8,128)(2,1)}, bf16[512,768]{1,0:T(8,128)(2,1)S(1)}, u32[]{:S(2)}, u32[]{:S(2)}) collective-permute-start(bf16[512,768]{1,0:T(8,128)(2,1)} %e_ref.3), channel_id=1, source_target_pairs={{0,1},{1,0},{2,3},{3,2},{4,5},{5,4},{6,7},{7,6},{8,9},{9,8},{10,11... | collective-permute-start | bytes 2359304 | tf_op jit(solution)/shard_map/ppermute | solution.py:260
  9.4 0.0 copy-start
  9.4 1.1 %copy-done = bf16[512,768]{1,0:T(8,128)(2,1)S(1)} copy-done((bf16[512,768]{1,0:T(8,128)(2,1)S(1)}, bf16[512,768]{1,0:T(8,128)(2,1)}, u32[]{:S(2)}) %copy-start) | copy-done | bytes 786456
  10.5 0.5 gram_own.1.refs_0_
  11.0 0.5 collective-permute-done.e_ref
  11.5 0.5 gram_both.1
  12.0 21.1 %all_to_all.15 = f32[32,1,5120]{2,1,0:T(1,128)S(1)} all-to-all(f32[32,1,5120]{2,1,0:T(1,128)S(1)} %bitcast.7), channel_id=1, replica_groups={{0,2,4,6,64,66,68,70,128,130,132,134,192,194,196,198,256,258,260,262,32..., dimensions={0} | all-to-all | bytes 1310720 | tf_op jit(solution)/shard_map/all_to_all | solution.py:256
  33.1 0.1 total_32_8.1
  33.2 14.9 %all_to_all.16 = f32[8,1,5120]{2,1,0:T(1,128)S(1)} all-to-all(f32[8,1,5120]{2,1,0:T(1,128)S(1)} %bitcast.12), channel_id=1, replica_groups={{0,8,16,24,32,40,48,56},{2,10,18,26,34,42,50,58},{4,12,20,28,36,44,52,6..., dimensions={0} | all-to-all | bytes 327680 | tf_op jit(solution)/shard_map/all_to_all | solution.py:256
  48.1 0.1 total_8_32.1
  48.1 0.0 copy-start.1
  48.1 18.7 %all_to_all.17 = f32[32,1,5120]{2,1,0:T(1,128)S(1)} all-to-all(f32[32,1,5120]{2,1,0:T(1,128)S(1)} %bitcast.9), channel_id=1, replica_groups={{0,2,4,6,64,66,68,70,128,130,132,134,192,194,196,198,256,258,260,262,32..., dimensions={0} | all-to-all | bytes 1310720 | tf_op jit(solution)/shard_map/all_to_all | solution.py:256
  66.9 6.0 %collective-permute-start.1 = (f32[1280,128]{1,0:T(8,128)S(1)}, f32[1280,128]{1,0:T(8,128)S(1)}, u32[]{:S(2)}, u32[]{:S(2)}) collective-permute-start(f32[1280,128]{1,0:T(8,128)S(1)} %bitcast.10), channel_id=1, source_target_pairs={{0,1},{1,0},{2,3},{3,2},{4,5},{5,4},{6,7},{7,6},{8,9},{9,8},{10,11... | collective-permute-start | bytes 1966088 | tf_op jit(solution)/shard_map/ppermute | solution.py:260
  72.9 1.5 %collective-permute-done.1.other_ref = f32[1280,128]{1,0:T(8,128)S(1)} collective-permute-done((f32[1280,128]{1,0:T(8,128)S(1)}, f32[1280,128]{1,0:T(8,128)S(1)}, u32[]{:S(2)}, u32[]{:S(2)}) %collective-permute-start.1) | collective-permute-done | bytes 655392 | tf_op jit(solution)/shard_map/ppermute | solution.py:260
  74.4 0.0 copy-done.1
  74.4 15.8 %whiten.1 = (bf16[512,768]{1,0:T(8,128)(2,1)}, f32[1,1]{1,0:T(1,128)}) custom-call(bf16[512,768]{1,0:T(8,128)(2,1)S(1)} %copy-done.1, f32[1280,128]{1,0:T(8,128)S(1)} %bitcast.11, f32[1280,128]{1,0:T(8,128)S(1)} %collective-permute-done.1.other_ref), custom_call_target="tpu_custom_call" | custom-call | flops 18119393280 | tf_op jit(solution)/shard_map/whiten/pallas_call | solution.py:264
Async XLA Ops:
  0.6 10.9 %collective-permute-start = (bf16[512,768]{1,0:T(8,128)(2,1)}, bf16[512,768]{1,0:T(8,128)(2,1)S(1)}, u32[]{:S(2)}, u32[]{:S(2)}) collective-permute-start(bf16[512,768]{1,0:T(8,128)(2,1)} %e_ref.3), channel_id=1, source_target_pairs={{0,1},{1,0},{2,3},{3,2},{4,5},{5,4},{6,7},{7,6},{8,9},{9,8},{10,11... | collective-permute-start | bytes 2359304 | tf_op jit(solution)/shard_map/ppermute | solution.py:260
  9.4 1.1 %copy-start = (bf16[512,768]{1,0:T(8,128)(2,1)S(1)}, bf16[512,768]{1,0:T(8,128)(2,1)}, u32[]{:S(2)}) copy-start(bf16[512,768]{1,0:T(8,128)(2,1)} %e_ref.3) | copy-start | bytes 2359300
  48.1 26.3 %copy-start.1 = (bf16[512,768]{1,0:T(8,128)(2,1)S(1)}, bf16[512,768]{1,0:T(8,128)(2,1)}, u32[]{:S(2)}) copy-start(bf16[512,768]{1,0:T(8,128)(2,1)} %e_ref.3) | copy-start | bytes 2359300
  66.9 7.6 %collective-permute-start.1 = (f32[1280,128]{1,0:T(8,128)S(1)}, f32[1280,128]{1,0:T(8,128)S(1)}, u32[]{:S(2)}, u32[]{:S(2)}) collective-permute-start(f32[1280,128]{1,0:T(8,128)S(1)} %bitcast.10), channel_id=1, source_target_pairs={{0,1},{1,0},{2,3},{3,2},{4,5},{5,4},{6,7},{7,6},{8,9},{9,8},{10,11... | collective-permute-start | bytes 1966088 | tf_op jit(solution)/shard_map/ppermute | solution.py:260

commit v6 on v5

--- a/solution.py
+++ b/solution.py
@@ -21,13 +21,13 @@
     place = {}
     at = [0, 0]
     for i in range(nb):
-        half = 0 if i < TILE // LANES else 1
         for j in range(i, nb):
             if j == i and i % 2:
                 continue
+            half = 0 if i < TILE // LANES and (i, j) != (1, nb - 1) else 1
             place[i, j] = (half, at[half])
             at[half] += LANES
-    return nb, place, at[1], max(at[0], at[1] + 16)
+    return nb, place, at[1], max(at[0], at[1] + nb + nb // 2)
 
 
 def upper(shape):
@@ -60,7 +60,8 @@
         put(place[i, i][1], jnp.where(keep, block(0, i), block(1, i + 1)))
         for r in range(2):
             for j in range(i + r + 1, nb):
-                put(place[i + r, j][1], block(r, j))
+                if (i + r, j) != (1, nb - 1):
+                    put(place[i + r, j][1], block(r, j))
 
     @pl.when(core == 0)
     def _():
@@ -70,6 +71,10 @@
     def _():
         for big in range(TILE, width, TILE):
             tile_row(big)
+        moved = lax.dot_general(
+            e_ref[:, LANES:TILE], e_ref[:, width - LANES :], (((0,), (0,)), ((), ())), preferred_element_type=F32
+        )
+        put(place[1, nb - 1][1], moved)
         e = e_ref[...].astype(F32)
         colsum = jnp.sum(e, axis=0, keepdims=True)
         lines = [colsum[:, k * LANES : (k + 1) * LANES] for k in range(nb)]
@@ -131,22 +136,18 @@
                     block = jnp.where(diag, line(nb + base // 2), jnp.where(keep, mirror, both))
             cov = block * inv - down[i] * means[j]
             squares = squares + (cov * cov) * (1.0 if i == j else 2.0)
-            s_ref[i * LANES : (i + 1) * LANES, j * LANES : (j + 1) * LANES] = cov
-    total = jnp.sum(jnp.sum(squares, axis=0, keepdims=True), axis=1, keepdims=True)
-    fro = jnp.sqrt(total + 1e-06)
-    rescale = 1.0 / fro
-    for i in range(nb):
-        for j in range(i, nb):
             at = (slice(i * LANES, (i + 1) * LANES), slice(j * LANES, (j + 1) * LANES))
-            s = s_ref[at] * rescale
-            s_ref[at] = s
-            sh[at], sl[at] = split(s)
+            s_ref[at] = cov
+            sh[at], sl[at] = split(cov)
             if i != j:
-                turned = jnp.transpose(s)
+                turned = jnp.transpose(cov)
                 ta = (at[1], at[0])
                 sh[ta], sl[ta] = split(turned)
                 if i // (TILE // LANES) == j // (TILE // LANES):
                     s_ref[ta] = turned
+    total = jnp.sum(jnp.sum(squares, axis=0, keepdims=True), axis=1, keepdims=True)
+    fro = jnp.sqrt(total + 1e-06)
+    rescale = 1.0 / fro
 
     nt = width // TILE
     pairs = [(i, j) for i in range(nt) for j in range(i, nt)]
@@ -173,11 +174,13 @@
         if i != j:
             h_ref[span(j), span(i)], l_ref[span(j), span(i)] = split(jnp.transpose(x))
 
-    def double_step(t_ref, th, tl, x_ref):
+    def double_step(t_ref, th, tl, scale, x_ref):
         for i, j in pairs:
             at = (span(i), span(j))
             t2 = squared(th, tl, i, j)
             t = t_ref[at]
+            if scale is not None:
+                t2, t = (t2 * scale) * scale, t * scale
             put(ah, al, i, j, t2)
             put(bh, bl, i, j, 0.0625 * t2 - 0.5625 * t)
             x_ref[at] = 1.6875 * t2 - 2.4375 * t
@@ -185,7 +188,7 @@
             at = (span(i), span(j))
             x_ref[at] = x_ref[at] + product(ah, al, bh, bl, i, j)
 
-    double_step(s_ref, sh, sl, r_ref)
+    double_step(s_ref, sh, sl, rescale, r_ref)
     for i, j in pairs:
         put(ah, al, i, j, r_ref[span(i), span(j)])
     for i, j in pairs:
@@ -193,10 +196,10 @@
         put(bh, bl, i, j, 4.5 * r_ref[at] + squared(ah, al, i, j))
     for i, j in pairs:
         at = (span(i), span(j))
-        q_ref[at] = 5.0625 * s_ref[at] + product(sh, sl, bh, bl, i, j)
+        q_ref[at] = (5.0625 * s_ref[at] + product(sh, sl, bh, bl, i, j)) * rescale
     for i, j in pairs:
         put(sh, sl, i, j, q_ref[span(i), span(j)])
-    double_step(q_ref, sh, sl, q_ref)
+    double_step(q_ref, sh, sl, None, q_ref)
     for i, j in pairs:
         put(ah, al, i, j, r_ref[span(i), span(j)])
         put(bh, bl, i, j, q_ref[span(i), span(j)])
@@ -217,7 +220,7 @@
         g = dot(w_ref[span(i), :], w_ref[:, span(j)])
         acc = acc + g * s_ref[span(i), span(j)] * (1.0 if i == j else 2.0)
     trace = jnp.sum(jnp.sum(acc, axis=0, keepdims=True), axis=1, keepdims=True)
-    en_ref[...] = trace * fro * (1.0 / width)
+    en_ref[...] = trace * (1.0 / width)
 
     mean = jnp.concatenate(means, axis=1)
     for r in range(0, rows_dev, TILE):
@@ -247,7 +250,7 @@
 
     planes, lines = groups(sizes)
     plane, line = len(planes[0]), len(lines[0])
-    rows = -(-need // (8 * plane)) * 8 * plane
+    rows = -(-need // plane) * plane
     half_type = jax.ShapeDtypeStruct((rows, LANES), F32)
 
     def exchange(x, members):

time: 90.5 us -> 89 us (0.983)
  blocking collectives: 54.7 us -> 53.7 us
    all_to_all x3, blocking collectives: 54.7 us -> 53.7 us  [exchange(): out = lax.all_to_all(y, AXES, 0, 0, axis_index_groups=members, tiled=True)]
where the time goes in v6:
time: 89 us; the launch traced here: 88.7 us
  blocking collectives  53.7 us (60%)
  Pallas kernels  16.6 us (19%)
  starting transfers between devices  14.7 us (17%)
  waiting for transfers between devices  1.87 us (2%)
  local copies, waits for them, and re-layouts  1.13 us (1%)
    all_to_all x3, blocking collectives, exchange(): out = lax.all_to_all(y, AXES, 0, 0, axis_index_groups=members, tiled=True)  53.7 us
    pallas_call x5, Pallas kernels, call(): pl.pallas_call(kernel, out_shape=out, in_specs=[vmem] * len(args), out_sp...  16.6 us
    ppermute x2, starting transfers between devices, swap(): return lax.ppermute(x, AXES[3], [(0, 1), (1, 0)])  14.7 us
    ppermute x2, waiting for transfers between devices, swap(): return lax.ppermute(x, AXES[3], [(0, 1), (1, 0)])  1.87 us
  transfers between devices with their start and end apart: 2, of which 2 were waited for; matrix products, arithmetic and copies ran while one was open for 0% of the time, Pallas kernels for 1%

profile of v6, /device:TPU:1, one launch (start us, length us, event | category | flops | bytes accessed | tf_op | source)
XLA Modules:
  0.0 88.7 jit_solution(10071502722766864115)
XLA Ops:
  0.6 8.7 %collective-permute-start = (bf16[512,768]{1,0:T(8,128)(2,1)}, bf16[512,768]{1,0:T(8,128)(2,1)S(1)}, u32[]{:S(2)}, u32[]{:S(2)}) collective-permute-start(bf16[512,768]{1,0:T(8,128)(2,1)} %e_ref.3), channel_id=1, source_target_pairs={{0,1},{1,0},{2,3},{3,2},{4,5},{5,4},{6,7},{7,6},{8,9},{9,8},{10,11... | collective-permute-start | bytes 2359304 | tf_op jit(solution)/shard_map/ppermute | solution.py:263
  9.4 0.0 copy-start
  9.4 1.1 %copy-done = bf16[512,768]{1,0:T(8,128)(2,1)S(1)} copy-done((bf16[512,768]{1,0:T(8,128)(2,1)S(1)}, bf16[512,768]{1,0:T(8,128)(2,1)}, u32[]{:S(2)}) %copy-start) | copy-done | bytes 786456
  10.5 0.5 gram_own.1.refs_0_
  11.1 0.4 collective-permute-done.e_ref
  11.5 0.6 gram_both.1
  12.0 20.7 %all_to_all.15 = f32[32,1,4736]{2,1,0:T(1,128)S(1)} all-to-all(f32[32,1,4736]{2,1,0:T(1,128)S(1)} %bitcast.9), channel_id=1, replica_groups={{0,2,4,6,64,66,68,70,128,130,132,134,192,194,196,198,256,258,260,262,32..., dimensions={0} | all-to-all | bytes 1212416 | tf_op jit(solution)/shard_map/all_to_all | solution.py:259
  32.8 0.1 total_32_8.1
  32.8 14.8 %all_to_all.16 = f32[8,1,4736]{2,1,0:T(1,128)S(1)} all-to-all(f32[8,1,4736]{2,1,0:T(1,128)S(1)} %bitcast.12), channel_id=1, replica_groups={{0,8,16,24,32,40,48,56},{2,10,18,26,34,42,50,58},{4,12,20,28,36,44,52,6..., dimensions={0} | all-to-all | bytes 303104 | tf_op jit(solution)/shard_map/all_to_all | solution.py:259
  47.6 0.1 total_8_32.1
  47.6 0.0 copy-start.1
  47.6 18.3 %all_to_all.17 = f32[32,1,4736]{2,1,0:T(1,128)S(1)} all-to-all(f32[32,1,4736]{2,1,0:T(1,128)S(1)} %bitcast.8), channel_id=1, replica_groups={{0,2,4,6,64,66,68,70,128,130,132,134,192,194,196,198,256,258,260,262,32..., dimensions={0} | all-to-all | bytes 1212416 | tf_op jit(solution)/shard_map/all_to_all | solution.py:259
  65.9 5.9 %collective-permute-start.1 = (f32[1184,128]{1,0:T(8,128)S(1)}, f32[1184,128]{1,0:T(8,128)S(1)}, u32[]{:S(2)}, u32[]{:S(2)}) collective-permute-start(f32[1184,128]{1,0:T(8,128)S(1)} %bitcast.10), channel_id=1, source_target_pairs={{0,1},{1,0},{2,3},{3,2},{4,5},{5,4},{6,7},{7,6},{8,9},{9,8},{10,11... | collective-permute-start | bytes 1818632 | tf_op jit(solution)/shard_map/ppermute | solution.py:263
  71.8 1.5 %collective-permute-done.1.other_ref = f32[1184,128]{1,0:T(8,128)S(1)} collective-permute-done((f32[1184,128]{1,0:T(8,128)S(1)}, f32[1184,128]{1,0:T(8,128)S(1)}, u32[]{:S(2)}, u32[]{:S(2)}) %collective-permute-start.1) | collective-permute-done | bytes 606240 | tf_op jit(solution)/shard_map/ppermute | solution.py:263
  73.3 0.0 copy-done.1
  73.3 15.4 %whiten.1 = (bf16[512,768]{1,0:T(8,128)(2,1)}, f32[1,1]{1,0:T(1,128)}) custom-call(bf16[512,768]{1,0:T(8,128)(2,1)S(1)} %copy-done.1, f32[1184,128]{1,0:T(8,128)S(1)} %bitcast.11, f32[1184,128]{1,0:T(8,128)S(1)} %collective-permute-done.1.other_ref), custom_call_target="tpu_custom_call" | custom-call | flops 18119393280 | tf_op jit(solution)/shard_map/whiten/pallas_call | solution.py:267
Async XLA Ops:
  0.6 10.9 %collective-permute-start = (bf16[512,768]{1,0:T(8,128)(2,1)}, bf16[512,768]{1,0:T(8,128)(2,1)S(1)}, u32[]{:S(2)}, u32[]{:S(2)}) collective-permute-start(bf16[512,768]{1,0:T(8,128)(2,1)} %e_ref.3), channel_id=1, source_target_pairs={{0,1},{1,0},{2,3},{3,2},{4,5},{5,4},{6,7},{7,6},{8,9},{9,8},{10,11... | collective-permute-start | bytes 2359304 | tf_op jit(solution)/shard_map/ppermute | solution.py:263
  9.4 1.1 %copy-start = (bf16[512,768]{1,0:T(8,128)(2,1)S(1)}, bf16[512,768]{1,0:T(8,128)(2,1)}, u32[]{:S(2)}) copy-start(bf16[512,768]{1,0:T(8,128)(2,1)} %e_ref.3) | copy-start | bytes 2359300
  47.6 25.6 %copy-start.1 = (bf16[512,768]{1,0:T(8,128)(2,1)S(1)}, bf16[512,768]{1,0:T(8,128)(2,1)}, u32[]{:S(2)}) copy-start(bf16[512,768]{1,0:T(8,128)(2,1)} %e_ref.3) | copy-start | bytes 2359300
  65.9 7.4 %collective-permute-start.1 = (f32[1184,128]{1,0:T(8,128)S(1)}, f32[1184,128]{1,0:T(8,128)S(1)}, u32[]{:S(2)}, u32[]{:S(2)}) collective-permute-start(f32[1184,128]{1,0:T(8,128)S(1)} %bitcast.10), channel_id=1, source_target_pairs={{0,1},{1,0},{2,3},{3,2},{4,5},{5,4},{6,7},{7,6},{8,9},{9,8},{10,11... | collective-permute-start | bytes 1818632 | tf_op jit(solution)/shard_map/ppermute | solution.py:263

commit v7 on v6

--- a/solution.py
+++ b/solution.py
@@ -181,12 +181,12 @@
             t = t_ref[at]
             if scale is not None:
                 t2, t = (t2 * scale) * scale, t * scale
-            put(ah, al, i, j, t2)
-            put(bh, bl, i, j, 0.0625 * t2 - 0.5625 * t)
-            x_ref[at] = 1.6875 * t2 - 2.4375 * t
+            v = t2 - 4.5 * t
+            put(ah, al, i, j, v)
+            x_ref[at] = 0.421875 * v - 0.5390625 * t
         for i, j in pairs:
             at = (span(i), span(j))
-            x_ref[at] = x_ref[at] + product(ah, al, bh, bl, i, j)
+            x_ref[at] = x_ref[at] + 0.0625 * squared(ah, al, i, j)
 
     double_step(s_ref, sh, sl, rescale, r_ref)
     for i, j in pairs:

time: 89 us -> 88.4 us (level)
  no operation moved by 1% of the time
where the time goes in v7:
time: 88.4 us; the launch traced here: 88 us
  blocking collectives  53.7 us (61%)
  Pallas kernels  16 us (18%)
  starting transfers between devices  14.7 us (17%)
  waiting for transfers between devices  1.87 us (2%)
  local copies, waits for them, and re-layouts  1.13 us (1%)
    all_to_all x3, blocking collectives, exchange(): out = lax.all_to_all(y, AXES, 0, 0, axis_index_groups=members, tiled=True)  53.7 us
    pallas_call x5, Pallas kernels, call(): pl.pallas_call(kernel, out_shape=out, in_specs=[vmem] * len(args), out_sp...  16 us
    ppermute x2, starting transfers between devices, swap(): return lax.ppermute(x, AXES[3], [(0, 1), (1, 0)])  14.7 us
    ppermute x2, waiting for transfers between devices, swap(): return lax.ppermute(x, AXES[3], [(0, 1), (1, 0)])  1.87 us
  transfers between devices with their start and end apart: 2, of which 2 were waited for; matrix products, arithmetic and copies ran while one was open for 0% of the time, Pallas kernels for 1%

profile of v7, /device:TPU:1, one launch (start us, length us, event | category | flops | bytes accessed | tf_op | source)
XLA Modules:
  0.0 88.0 jit_solution(9258813068455081212)
XLA Ops:
  0.6 8.7 %collective-permute-start = (bf16[512,768]{1,0:T(8,128)(2,1)}, bf16[512,768]{1,0:T(8,128)(2,1)S(1)}, u32[]{:S(2)}, u32[]{:S(2)}) collective-permute-start(bf16[512,768]{1,0:T(8,128)(2,1)} %e_ref.3), channel_id=1, source_target_pairs={{0,1},{1,0},{2,3},{3,2},{4,5},{5,4},{6,7},{7,6},{8,9},{9,8},{10,11... | collective-permute-start | bytes 2359304 | tf_op jit(solution)/shard_map/ppermute | solution.py:263
  9.4 0.0 copy-start
  9.4 1.1 %copy-done = bf16[512,768]{1,0:T(8,128)(2,1)S(1)} copy-done((bf16[512,768]{1,0:T(8,128)(2,1)S(1)}, bf16[512,768]{1,0:T(8,128)(2,1)}, u32[]{:S(2)}) %copy-start) | copy-done | bytes 786456
  10.5 0.5 gram_own.1.refs_0_
  11.1 0.4 collective-permute-done.e_ref
  11.5 0.6 gram_both.1
  12.0 20.7 %all_to_all.15 = f32[32,1,4736]{2,1,0:T(1,128)S(1)} all-to-all(f32[32,1,4736]{2,1,0:T(1,128)S(1)} %bitcast.9), channel_id=1, replica_groups={{0,2,4,6,64,66,68,70,128,130,132,134,192,194,196,198,256,258,260,262,32..., dimensions={0} | all-to-all | bytes 1212416 | tf_op jit(solution)/shard_map/all_to_all | solution.py:259
  32.8 0.1 total_32_8.1
  32.8 14.8 %all_to_all.16 = f32[8,1,4736]{2,1,0:T(1,128)S(1)} all-to-all(f32[8,1,4736]{2,1,0:T(1,128)S(1)} %bitcast.12), channel_id=1, replica_groups={{0,8,16,24,32,40,48,56},{2,10,18,26,34,42,50,58},{4,12,20,28,36,44,52,6..., dimensions={0} | all-to-all | bytes 303104 | tf_op jit(solution)/shard_map/all_to_all | solution.py:259
  47.6 0.1 total_8_32.1
  47.6 0.0 copy-start.1
  47.6 18.3 %all_to_all.17 = f32[32,1,4736]{2,1,0:T(1,128)S(1)} all-to-all(f32[32,1,4736]{2,1,0:T(1,128)S(1)} %bitcast.8), channel_id=1, replica_groups={{0,2,4,6,64,66,68,70,128,130,132,134,192,194,196,198,256,258,260,262,32..., dimensions={0} | all-to-all | bytes 1212416 | tf_op jit(solution)/shard_map/all_to_all | solution.py:259
  65.9 5.9 %collective-permute-start.1 = (f32[1184,128]{1,0:T(8,128)S(1)}, f32[1184,128]{1,0:T(8,128)S(1)}, u32[]{:S(2)}, u32[]{:S(2)}) collective-permute-start(f32[1184,128]{1,0:T(8,128)S(1)} %bitcast.10), channel_id=1, source_target_pairs={{0,1},{1,0},{2,3},{3,2},{4,5},{5,4},{6,7},{7,6},{8,9},{9,8},{10,11... | collective-permute-start | bytes 1818632 | tf_op jit(solution)/shard_map/ppermute | solution.py:263
  71.8 1.5 %collective-permute-done.1.other_ref = f32[1184,128]{1,0:T(8,128)S(1)} collective-permute-done((f32[1184,128]{1,0:T(8,128)S(1)}, f32[1184,128]{1,0:T(8,128)S(1)}, u32[]{:S(2)}, u32[]{:S(2)}) %collective-permute-start.1) | collective-permute-done | bytes 606240 | tf_op jit(solution)/shard_map/ppermute | solution.py:263
  73.3 0.0 copy-done.1
  73.3 14.8 %whiten.1 = (bf16[512,768]{1,0:T(8,128)(2,1)}, f32[1,1]{1,0:T(1,128)}) custom-call(bf16[512,768]{1,0:T(8,128)(2,1)S(1)} %copy-done.1, f32[1184,128]{1,0:T(8,128)S(1)} %bitcast.11, f32[1184,128]{1,0:T(8,128)S(1)} %collective-permute-done.1.other_ref), custom_call_target="tpu_custom_call" | custom-call | flops 18119393280 | tf_op jit(solution)/shard_map/whiten/pallas_call | solution.py:267
Async XLA Ops:
  0.6 10.9 %collective-permute-start = (bf16[512,768]{1,0:T(8,128)(2,1)}, bf16[512,768]{1,0:T(8,128)(2,1)S(1)}, u32[]{:S(2)}, u32[]{:S(2)}) collective-permute-start(bf16[512,768]{1,0:T(8,128)(2,1)} %e_ref.3), channel_id=1, source_target_pairs={{0,1},{1,0},{2,3},{3,2},{4,5},{5,4},{6,7},{7,6},{8,9},{9,8},{10,11... | collective-permute-start | bytes 2359304 | tf_op jit(solution)/shard_map/ppermute | solution.py:263
  9.4 1.1 %copy-start = (bf16[512,768]{1,0:T(8,128)(2,1)S(1)}, bf16[512,768]{1,0:T(8,128)(2,1)}, u32[]{:S(2)}) copy-start(bf16[512,768]{1,0:T(8,128)(2,1)} %e_ref.3) | copy-start | bytes 2359300
  47.6 25.6 %copy-start.1 = (bf16[512,768]{1,0:T(8,128)(2,1)S(1)}, bf16[512,768]{1,0:T(8,128)(2,1)}, u32[]{:S(2)}) copy-start(bf16[512,768]{1,0:T(8,128)(2,1)} %e_ref.3) | copy-start | bytes 2359300
  65.9 7.4 %collective-permute-start.1 = (f32[1184,128]{1,0:T(8,128)S(1)}, f32[1184,128]{1,0:T(8,128)S(1)}, u32[]{:S(2)}, u32[]{:S(2)}) collective-permute-start(f32[1184,128]{1,0:T(8,128)S(1)} %bitcast.10), channel_id=1, source_target_pairs={{0,1},{1,0},{2,3},{3,2},{4,5},{5,4},{6,7},{7,6},{8,9},{9,8},{10,11... | collective-permute-start | bytes 1818632 | tf_op jit(solution)/shard_map/ppermute | solution.py:263

commit v8 on v7

--- a/solution.py
+++ b/solution.py
@@ -102,7 +102,7 @@
     return hi, lo
 
 
-def whiten_kernel(rows_total, e_ref, own_ref, other_ref, o_ref, en_ref, half_ref, s_ref, r_ref, q_ref, sh, sl, ah, al, bh, bl, w_ref):
+def whiten_kernel(rows_total, e_ref, own_ref, other_ref, o_ref, en_ref, half_ref, s_ref, r_ref, q_ref, sh, sl, ah, al, bh, bl, w_ref, white_ref, sems):
     rows_dev, width = e_ref.shape
     nb, place, tail, _ = layout(width)
     inv = 1.0 / rows_total
@@ -140,11 +140,10 @@
             s_ref[at] = cov
             sh[at], sl[at] = split(cov)
             if i != j:
-                turned = jnp.transpose(cov)
                 ta = (at[1], at[0])
-                sh[ta], sl[ta] = split(turned)
+                sh[ta], sl[ta] = jnp.transpose(sh[at]), jnp.transpose(sl[at])
                 if i // (TILE // LANES) == j // (TILE // LANES):
-                    s_ref[ta] = turned
+                    s_ref[ta] = jnp.transpose(cov)
     total = jnp.sum(jnp.sum(squares, axis=0, keepdims=True), axis=1, keepdims=True)
     fro = jnp.sqrt(total + 1e-06)
     rescale = 1.0 / fro
@@ -170,9 +169,10 @@
         return dot(xh[a, :], xh[:, a]) + (cross + jnp.transpose(cross))
 
     def put(h_ref, l_ref, i, j, x):
-        h_ref[span(i), span(j)], l_ref[span(i), span(j)] = split(x)
+        hi, lo = split(x)
+        h_ref[span(i), span(j)], l_ref[span(i), span(j)] = hi, lo
         if i != j:
-            h_ref[span(j), span(i)], l_ref[span(j), span(i)] = split(jnp.transpose(x))
+            h_ref[span(j), span(i)], l_ref[span(j), span(i)] = jnp.transpose(hi), jnp.transpose(lo)
 
     def double_step(t_ref, th, tl, scale, x_ref):
         for i, j in pairs:
@@ -213,19 +213,28 @@
         w = (z * root).astype(BF16)
         w_ref[at] = w
         if i != j:
-            w_ref[span(j), span(i)] = jnp.transpose(w.astype(F32)).astype(BF16)
+            w_ref[span(j), span(i)] = jnp.transpose(w)
+
+    mean = jnp.concatenate(means, axis=1)
+    copies = []
+    for n, r in enumerate(range(0, rows_dev, LANES)):
+        c = (e_ref[r : r + LANES, :].astype(F32) - mean).astype(BF16)
+        white_ref[r : r + LANES, :] = dot(c, w_ref[...]).astype(BF16)
+        if copies:
+            copies[-1].start()
+        piece = pl.ds(r, LANES)
+        copies.append(pltpu.make_async_copy(white_ref.at[piece, :], o_ref.at[piece, :], sems.at[n]))
 
     acc = jnp.zeros((TILE, TILE), F32)
-    for i, j in pairs:
+    for n, (i, j) in enumerate(pairs):
         g = dot(w_ref[span(i), :], w_ref[:, span(j)])
         acc = acc + g * s_ref[span(i), span(j)] * (1.0 if i == j else 2.0)
+        if n == 0:
+            copies[-1].start()
     trace = jnp.sum(jnp.sum(acc, axis=0, keepdims=True), axis=1, keepdims=True)
     en_ref[...] = trace * (1.0 / width)
-
-    mean = jnp.concatenate(means, axis=1)
-    for r in range(0, rows_dev, TILE):
-        c = (e_ref[r : r + TILE, :].astype(F32) - mean).astype(BF16)
-        o_ref[r : r + TILE, :] = dot(c, w_ref[...]).astype(BF16)
+    for copy in copies:
+        copy.wait()
 
 
 def groups(sizes):
@@ -262,13 +271,13 @@
     def swap(x):
         return lax.ppermute(x, AXES[3], [(0, 1), (1, 0)])
 
-    def call(kernel, out, name, *args, flops=0, mib=8, **rest):
+    def call(kernel, out, name, *args, flops=0, mib=8, out_specs=None, **rest):
         cost = pl.CostEstimate(flops=flops, bytes_accessed=0, transcendentals=0)
         return pl.pallas_call(
             kernel,
             out_shape=out,
             in_specs=[vmem] * len(args),
-            out_specs=jax.tree.map(lambda _: vmem, out),
+            out_specs=out_specs or jax.tree.map(lambda _: vmem, out),
             cost_estimate=cost,
             compiler_params=pltpu.CompilerParams(vmem_limit_bytes=mib << 20),
             name=name,
@@ -297,9 +306,11 @@
         swap(half),
         flops=40 * width**3,
         mib=32,
+        out_specs=(pl.BlockSpec(memory_space=pl.ANY), vmem),
         scratch_shapes=[pltpu.VMEM((2, rows, LANES), F32)]
         + [pltpu.VMEM(square, F32)] * 3
-        + [pltpu.VMEM(square, BF16)] * 7,
+        + [pltpu.VMEM(square, BF16)] * 7
+        + [pltpu.VMEM((rows_dev, width), BF16), pltpu.SemaphoreType.DMA((rows_dev // LANES,))],
     )
     return whitened, energy.reshape(())
 

time: 88.4 us -> 88.1 us (level)
  no operation moved by 1% of the time
where the time goes in v8:
time: 88.1 us; the launch traced here: 87.8 us
  blocking collectives  53.7 us (61%)
  Pallas kernels  15.5 us (18%)
  starting transfers between devices  14.7 us (17%)
  waiting for transfers between devices  1.87 us (2%)
  local copies, waits for them, and re-layouts  1.13 us (1%)
    all_to_all x3, blocking collectives, exchange(): out = lax.all_to_all(y, AXES, 0, 0, axis_index_groups=members, tiled=True)  53.7 us
    pallas_call x5, Pallas kernels, call(): pl.pallas_call(kernel, out_shape=out, in_specs=[vmem] * len(args), out_sp...  15.5 us
    ppermute x2, starting transfers between devices, swap(): return lax.ppermute(x, AXES[3], [(0, 1), (1, 0)])  14.7 us
    ppermute x2, waiting for transfers between devices, swap(): return lax.ppermute(x, AXES[3], [(0, 1), (1, 0)])  1.87 us
  transfers between devices with their start and end apart: 2, of which 2 were waited for; matrix products, arithmetic and copies ran while one was open for 0% of the time, Pallas kernels for 1%

profile of v8, /device:TPU:1, one launch (start us, length us, event | category | flops | bytes accessed | tf_op | source)
XLA Modules:
  0.0 87.8 jit_solution(10896041118548786706)
XLA Ops:
  0.6 8.7 %collective-permute-start = (bf16[512,768]{1,0:T(8,128)(2,1)}, bf16[512,768]{1,0:T(8,128)(2,1)S(1)}, u32[]{:S(2)}, u32[]{:S(2)}) collective-permute-start(bf16[512,768]{1,0:T(8,128)(2,1)} %e_ref.3), channel_id=1, source_target_pairs={{0,1},{1,0},{2,3},{3,2},{4,5},{5,4},{6,7},{7,6},{8,9},{9,8},{10,11... | collective-permute-start | bytes 2359304 | tf_op jit(solution)/shard_map/ppermute | solution.py:272
  9.4 0.0 copy-start
  9.4 1.1 %copy-done = bf16[512,768]{1,0:T(8,128)(2,1)S(1)} copy-done((bf16[512,768]{1,0:T(8,128)(2,1)S(1)}, bf16[512,768]{1,0:T(8,128)(2,1)}, u32[]{:S(2)}) %copy-start) | copy-done | bytes 786456
  10.5 0.5 gram_own.1.refs_0_
  11.1 0.4 collective-permute-done.e_ref
  11.5 0.6 gram_both.1
  12.0 20.7 %all_to_all.15 = f32[32,1,4736]{2,1,0:T(1,128)S(1)} all-to-all(f32[32,1,4736]{2,1,0:T(1,128)S(1)} %bitcast.9), channel_id=1, replica_groups={{0,2,4,6,64,66,68,70,128,130,132,134,192,194,196,198,256,258,260,262,32..., dimensions={0} | all-to-all | bytes 1212416 | tf_op jit(solution)/shard_map/all_to_all | solution.py:268
  32.8 0.1 total_32_8.1
  32.8 14.8 %all_to_all.16 = f32[8,1,4736]{2,1,0:T(1,128)S(1)} all-to-all(f32[8,1,4736]{2,1,0:T(1,128)S(1)} %bitcast.12), channel_id=1, replica_groups={{0,8,16,24,32,40,48,56},{2,10,18,26,34,42,50,58},{4,12,20,28,36,44,52,6..., dimensions={0} | all-to-all | bytes 303104 | tf_op jit(solution)/shard_map/all_to_all | solution.py:268
  47.6 0.1 total_8_32.1
  47.6 0.0 copy-start.1
  47.6 18.3 %all_to_all.17 = f32[32,1,4736]{2,1,0:T(1,128)S(1)} all-to-all(f32[32,1,4736]{2,1,0:T(1,128)S(1)} %bitcast.8), channel_id=1, replica_groups={{0,2,4,6,64,66,68,70,128,130,132,134,192,194,196,198,256,258,260,262,32..., dimensions={0} | all-to-all | bytes 1212416 | tf_op jit(solution)/shard_map/all_to_all | solution.py:268
  65.9 5.9 %collective-permute-start.1 = (f32[1184,128]{1,0:T(8,128)S(1)}, f32[1184,128]{1,0:T(8,128)S(1)}, u32[]{:S(2)}, u32[]{:S(2)}) collective-permute-start(f32[1184,128]{1,0:T(8,128)S(1)} %bitcast.10), channel_id=1, source_target_pairs={{0,1},{1,0},{2,3},{3,2},{4,5},{5,4},{6,7},{7,6},{8,9},{9,8},{10,11... | collective-permute-start | bytes 1818632 | tf_op jit(solution)/shard_map/ppermute | solution.py:272
  71.8 1.5 %collective-permute-done.1.other_ref = f32[1184,128]{1,0:T(8,128)S(1)} collective-permute-done((f32[1184,128]{1,0:T(8,128)S(1)}, f32[1184,128]{1,0:T(8,128)S(1)}, u32[]{:S(2)}, u32[]{:S(2)}) %collective-permute-start.1) | collective-permute-done | bytes 606240 | tf_op jit(solution)/shard_map/ppermute | solution.py:272
  73.3 0.0 copy-done.1
  73.3 14.3 %whiten.1 = (bf16[512,768]{1,0:T(8,128)(2,1)}, f32[1,1]{1,0:T(1,128)}) custom-call(bf16[512,768]{1,0:T(8,128)(2,1)S(1)} %copy-done.1, f32[1184,128]{1,0:T(8,128)S(1)} %bitcast.11, f32[1184,128]{1,0:T(8,128)S(1)} %collective-permute-done.1.other_ref), custom_call_target="tpu_custom_call" | custom-call | flops 18119393280 | tf_op jit(solution)/shard_map/whiten/pallas_call | solution.py:276
Async XLA Ops:
  0.6 10.9 %collective-permute-start = (bf16[512,768]{1,0:T(8,128)(2,1)}, bf16[512,768]{1,0:T(8,128)(2,1)S(1)}, u32[]{:S(2)}, u32[]{:S(2)}) collective-permute-start(bf16[512,768]{1,0:T(8,128)(2,1)} %e_ref.3), channel_id=1, source_target_pairs={{0,1},{1,0},{2,3},{3,2},{4,5},{5,4},{6,7},{7,6},{8,9},{9,8},{10,11... | collective-permute-start | bytes 2359304 | tf_op jit(solution)/shard_map/ppermute | solution.py:272
  9.4 1.1 %copy-start = (bf16[512,768]{1,0:T(8,128)(2,1)S(1)}, bf16[512,768]{1,0:T(8,128)(2,1)}, u32[]{:S(2)}) copy-start(bf16[512,768]{1,0:T(8,128)(2,1)} %e_ref.3) | copy-start | bytes 2359300
  47.6 25.6 %copy-start.1 = (bf16[512,768]{1,0:T(8,128)(2,1)S(1)}, bf16[512,768]{1,0:T(8,128)(2,1)}, u32[]{:S(2)}) copy-start(bf16[512,768]{1,0:T(8,128)(2,1)} %e_ref.3) | copy-start | bytes 2359300
  65.9 7.4 %collective-permute-start.1 = (f32[1184,128]{1,0:T(8,128)S(1)}, f32[1184,128]{1,0:T(8,128)S(1)}, u32[]{:S(2)}, u32[]{:S(2)}) collective-permute-start(f32[1184,128]{1,0:T(8,128)S(1)} %bitcast.10), channel_id=1, source_target_pairs={{0,1},{1,0},{2,3},{3,2},{4,5},{5,4},{6,7},{7,6},{8,9},{9,8},{10,11... | collective-permute-start | bytes 1818632 | tf_op jit(solution)/shard_map/ppermute | solution.py:272
